TPU v7x, 256 devices: a whole 4x4x8 slice. The times are simulated.
256 devices in a mesh: leaf: 16 (over z, core), pts: 16 (over x, y).
Axes of the slice: x: 4, y: 4, z: 8, core: 2. Of those that a mesh axis runs over, the one named last changes fastest.
Arguments:
- leaf_solved: float32 [262144, 256], P(('leaf', 'pts')), may hold values from -6 to 6
- points: float32 [3, 262144], P(None, ('leaf', 'pts')), may hold values from -8 to 8
- panel_top: float32 [262144, 256], P(('leaf', 'pts')), may hold values from -0.015625 to 0.015625
- panel_mid: float32 [262144, 256], P(('leaf', 'pts')), may hold values from -0.0234375 to 0.0234375
- panel_low: float32 [262144, 256], P(('leaf', 'pts')), may hold values from -0.03125 to 0.03125
- solved_top: float32 [262144, 256], P(('leaf', 'pts')), may hold values from -0.046875 to 0.046875
- solved_mid: float32 [262144, 256], P(('leaf', 'pts')), may hold values from -0.046875 to 0.046875
- solved_low: float32 [262144, 256], P(('leaf', 'pts')), may hold values from -0.046875 to 0.046875
- skeleton_top: int32 [2, 256], replicated, may hold values from 0 to 262143, as said below
- skeleton_mid: int32 [4, 256], replicated, may hold values from 0 to 262143, as said below
- skeleton_low: int32 [8, 256], replicated, may hold values from 0 to 262143, as said below
Outputs:
- solution: float32 [262144, 256], P(('leaf', 'pts'))
Inputs may be any that keep to these rules, and one draw needn't show every extreme that they name: `skeleton_top`: row k holds 256 different indices of points of child k of the level, all between k * 131072 and (k + 1) * 131072 - 1. `skeleton_mid`: row k holds 256 different indices of points of child k of the level, all between k * 65536 and (k + 1) * 65536 - 1. `skeleton_low`: row k holds 256 different indices of points of child k of the level, all between k * 32768 and (k + 1) * 32768 - 1.
All inputs are finite; a program needn't handle non-finite values.
Results may differ from a plain program's by a relative error of at most 0.00005.
Values sent between devices are 32-bit elements; how exact they have to be, the bound alone decides.
No kernel may reach another device: no remote copies, remote signals or barrier semaphores. Data moves between devices by JAX's collectives and lax.ppermute only.
A program may use at most 128 MiB of HBM per device.

v0:
```python
import functools

import jax
import jax.numpy as jnp
from jax import lax
from jax.experimental import pallas as pl
from jax.experimental.pallas import tpu as pltpu
from jax.sharding import PartitionSpec as P


F32 = jnp.float32
BEST = lax.Precision.HIGHEST


def dot(a, b):
    return jnp.dot(a, b, preferred_element_type=F32)


def dot_t(a, b):
    return lax.dot_general(a, b, (((1,), (1,)), ((), ())), preferred_element_type=F32)


def cut(value):
    big = value.astype(jnp.bfloat16)
    return big, (value - big.astype(F32)).astype(jnp.bfloat16)


def mm3(a, b, by=dot):
    (a1, a2), (b1, b2) = a, b
    return by(a1, b1) + (by(a1, b2) + by(a2, b1))


def product_kernel(count, core_ref, *refs):
    sources = refs[: count + 3]
    keep_ref, send_ref, acc, side1, side2, piece1, piece2, come = refs[count + 3 : count + 11]
    held = refs[count + 11 :]
    rows, rank = held[0].shape
    chunk = rank
    loads = []
    for i in range(rows // chunk):
        at = slice(i * chunk, (i + 1) * chunk)
        for k, (source, place_) in enumerate(zip(sources, held)):
            load = pltpu.make_async_copy(source.at[at, :], place_.at[at, :], come.at[i, k])
            load.start()
            loads.append(load)
    for i in range(rows // chunk):
        at = slice(i * chunk, (i + 1) * chunk)
        for load in loads[i * (count + 3) : (i + 1) * (count + 3)]:
            load.wait()
        for b in range(count):
            band = slice(b * rank, (b + 1) * rank)
            side1[band, at], side2[band, at] = cut(jnp.transpose(held[b][at, :]))
        for k in range(3):
            band = slice(k * rank, (k + 1) * rank)
            piece1[at, band], piece2[at, band] = cut(held[count + k][at, :])
    for k in range(3):
        band = slice(k * rank, (k + 1) * rank)
        one, two = piece1[:, band], piece2[:, band]
        acc[:, band] = dot(side1[...], one) + (dot(side1[...], two) + dot(side2[...], one))
    core = core_ref[0]
    for ref, which in ((keep_ref, core), (send_ref, 1 - core)):
        for p in range(keep_ref.shape[0]):
            for b in range(count):
                row = pl.multiple_of(b * rank + which * (rank // 2) + p * 8, 8)
                ref[p, :, b * 3 * rank : (b + 1) * 3 * rank] = acc[pl.ds(row, 8), :]


def call_product(core, columns, panels, many):
    rows, rank = panels[0].shape
    count = len(columns)
    half = jax.ShapeDtypeStruct((many, 8, count * 3 * rank), F32)
    vm = pl.BlockSpec(memory_space=pltpu.VMEM)
    return pl.pallas_call(
        functools.partial(product_kernel, count),
        out_shape=(half, half),
        in_specs=[pl.BlockSpec(memory_space=pltpu.SMEM)] + [pl.BlockSpec(memory_space=pltpu.HBM)] * (count + 3),
        out_specs=(vm, vm),
        scratch_shapes=[pltpu.VMEM((count * rank, 3 * rank), F32)]
        + [pltpu.VMEM((count * rank, rows), jnp.bfloat16)] * 2
        + [pltpu.VMEM((rows, 3 * rank), jnp.bfloat16)] * 2
        + [pltpu.SemaphoreType.DMA((rows // rank, count + 3))]
        + [pltpu.VMEM((rows, rank), F32)] * (count + 3),
        cost_estimate=pl.CostEstimate(
            flops=count * 18 * rows * rank * rank, bytes_accessed=4 * rows * rank * (count + 3), transcendentals=0
        ),
        compiler_params=pltpu.CompilerParams(vmem_limit_bytes=60 * 1024 * 1024),
    )(core, *columns, *panels)


def fro2(value):
    return jnp.sum(value * value)


def inverse_into(n_ref, y_ref, e_ref):
    rank = n_ref.shape[0]
    row = lax.broadcasted_iota(jnp.int32, (rank, rank), 0)
    col = lax.broadcasted_iota(jnp.int32, (rank, rank), 1)
    ident = jnp.where(row == col, 1.0, 0.0).astype(F32)
    y_ref[...] = ident + n_ref[...]
    e_ref[...] = n_ref[...]

    @pl.loop(0, 2)
    def _(step):
        before = cut(e_ref[...])
        square = mm3(before, before)
        e_ref[...] = square
        y = y_ref[...]
        y_ref[...] = y + mm3(cut(y), cut(square))

    def residual():
        y = y_ref[...]
        left = ident - y + mm3(cut(y), cut(n_ref[...]))
        e_ref[...] = left
        return fro2(left)

    def improve():
        y = y_ref[...]
        y_ref[...] = y + mm3(cut(e_ref[...]), cut(y))

    size = residual()
    good = size < 0.25

    @pl.when(jnp.logical_not(good))
    def _():
        system = ident - n_ref[...]
        most = jnp.max(jnp.sum(jnp.abs(system), axis=0, keepdims=True))
        most = most * jnp.max(jnp.sum(jnp.abs(system), axis=1, keepdims=True))
        y_ref[...] = jnp.transpose(system) / most
        residual()

    def unfinished(state):
        count, now, before = state
        stuck = jnp.logical_and(now < 0.1, now > 0.25 * before)
        return jnp.logical_and(count < 120, jnp.logical_not(jnp.logical_or(now < 4e-6, stuck)))

    def better(state):
        count, now, _ = state
        improve()
        return count + 1, residual(), now

    lax.while_loop(unfinished, better, (jnp.int32(0), jnp.where(good, size, F32(1e30)), F32(1e35)))
    improve()


def couple_of(spots):
    own = jnp.transpose(spots)
    total = None
    for d in range(3):
        spread = own[:, d : d + 1] - spots[3 + d : 4 + d, :]
        total = spread * spread if total is None else total + spread * spread
    return jnp.exp(-0.5 * total)


def place(core_ref, mine_ref, theirs_ref, full_ref):
    half = mine_ref.shape[0]
    core = core_ref[0]
    full_ref[pl.ds(pl.multiple_of(core * half, half), half), :] = mine_ref[...]
    full_ref[pl.ds(pl.multiple_of((1 - core) * half, half), half), :] = theirs_ref[...]


def spots_of(mine_ref, theirs_ref, at):
    rank = 2 * mine_ref.shape[0]
    total = None
    for ref in (mine_ref, theirs_ref):
        for q in range(rank // 16):
            some = ref[q * 8 : q * 8 + 8, at : at + rank]
            total = some if total is None else total + some
    return total


def level_kernel(at, core_ref, mine_ref, theirs_ref, own_ref, other_ref, ans_ref, next_ref, full, n, y, e):
    rank = full.shape[0]
    gram_at, upper_at, upper, gram_o_at, spot_at = at
    place(core_ref, mine_ref, theirs_ref, full)
    couple = couple_of(spots_of(mine_ref, theirs_ref, spot_at))
    couple_t = jnp.transpose(couple)
    gram = full[:, gram_at : gram_at + rank]
    gram_o = full[:, gram_o_at : gram_o_at + rank]
    c, c_t = cut(couple), cut(couple_t)
    far = cut(mm3(cut(gram_o), c_t))
    n[...] = mm3(cut(mm3(cut(gram), c)), far)
    inverse_into(n, y, e)
    target = mm3(cut(other_ref[...]), c_t) - mm3(cut(mm3(cut(own_ref[:, :rank]), c)), far)
    ans = mm3(cut(target), cut(y[...]))
    ans_ref[...] = ans
    next_ref[...] = own_ref[:, rank : rank + upper] - mm3(cut(ans), cut(full[:, upper_at : upper_at + upper]))


def call_level(core, mine, theirs, own, other, at):
    rank = 2 * mine.shape[0]
    rows, upper = own.shape[0], at[2]
    vm = pl.BlockSpec(memory_space=pltpu.VMEM)
    return pl.pallas_call(
        functools.partial(level_kernel, at),
        out_shape=(
            jax.ShapeDtypeStruct((rows, rank), F32),
            jax.ShapeDtypeStruct((rows, upper), F32),
        ),
        in_specs=[pl.BlockSpec(memory_space=pltpu.SMEM), vm, vm, vm, vm],
        out_specs=(vm, vm),
        scratch_shapes=[pltpu.VMEM((rank, mine.shape[1]), F32)] + [pltpu.VMEM((rank, rank), F32)] * 3,
        cost_estimate=pl.CostEstimate(
            flops=80 * 2 * rank**3, bytes_accessed=4 * rank * mine.shape[1], transcendentals=rank * rank
        ),
        compiler_params=pltpu.CompilerParams(vmem_limit_bytes=16 * 1024 * 1024),
    )(core, mine, theirs, own, other)


def top_kernel(core_ref, mine_ref, theirs_ref, *refs):
    held, out_ref = refs[:4], refs[4]
    full, n, y, e, stacked, result, go = refs[5:]
    rank = full.shape[0]
    place(core_ref, mine_ref, theirs_ref, full)
    part = lambda k: full[:, k * rank : (k + 1) * rank]
    couple = couple_of(spots_of(mine_ref, theirs_ref, 4 * rank))
    couple_t = jnp.transpose(couple)
    c, c_t = cut(couple), cut(couple_t)
    far = cut(mm3(cut(part(2)), c_t))
    n[...] = mm3(cut(mm3(cut(part(0)), c)), far)
    inverse_into(n, y, e)
    target = mm3(cut(part(3)), c_t) - mm3(cut(mm3(cut(part(1)), c)), far)
    top = cut(mm3(cut(target), cut(y[...])))
    mid = cut(part(6) - mm3(top, cut(part(5))))
    low = cut(part(9) - mm3(top, cut(part(8))) - mm3(mid, cut(part(7))))
    for k, (one, two) in enumerate((top, mid, low)):
        stacked[0, :, k * rank : (k + 1) * rank] = one
        stacked[1, :, k * rank : (k + 1) * rank] = two
    rows = result.shape[0]
    chunk = rows // 4
    stores = []
    for i in range(4):
        at = slice(i * chunk, (i + 1) * chunk)
        total = held[0][at, :]
        for k in range(3):
            lanes = slice(k * rank, (k + 1) * rank)
            total = total - mm3(cut(held[1 + k][at, :]), (stacked[0, :, lanes], stacked[1, :, lanes]), dot_t)
        result[at, :] = total
        store = pltpu.make_async_copy(result.at[at, :], out_ref.at[at, :], go.at[i])
        store.start()
        stores.append(store)
    for store in stores:
        store.wait()


def call_top(core, mine, theirs, carry):
    rank = 2 * mine.shape[0]
    rows = carry[0].shape[0]
    vm = pl.BlockSpec(memory_space=pltpu.VMEM)
    far = pl.BlockSpec(memory_space=pltpu.HBM)
    return pl.pallas_call(
        top_kernel,
        out_shape=jax.ShapeDtypeStruct((rows, rank), F32),
        in_specs=[pl.BlockSpec(memory_space=pltpu.SMEM), vm] * 1 + [vm] * 5,
        out_specs=far,
        scratch_shapes=[pltpu.VMEM((rank, mine.shape[1]), F32)]
        + [pltpu.VMEM((rank, rank), F32)] * 3
        + [pltpu.VMEM((2, rank, 3 * rank), jnp.bfloat16), pltpu.VMEM((rows, rank), F32)]
        + [pltpu.SemaphoreType.DMA((4,))],
        cost_estimate=pl.CostEstimate(
            flops=100 * 2 * rank**3, bytes_accessed=4 * rank * mine.shape[1] + 20 * rows * rank, transcendentals=rank * rank
        ),
        compiler_params=pltpu.CompilerParams(vmem_limit_bytes=32 * 1024 * 1024),
    )(core, mine, theirs, *carry)


def swap(value, mask):
    count = lax.axis_size("leaf")
    return lax.ppermute(value, "leaf", [(i, i ^ mask) for i in range(count)])


def to_all(piece):
    return jnp.broadcast_to(piece, (lax.axis_size("pts"), *piece.shape))


def exchanged(pieces):
    return lax.all_to_all(pieces, "pts", 0, 0, tiled=True)


def spread_to_all(piece):
    return exchanged(to_all(piece)).reshape(-1, piece.shape[-1])


def per_device(
    leaf_solved,
    points,
    panel_top,
    panel_mid,
    panel_low,
    solved_top,
    solved_mid,
    solved_low,
    skeleton_top,
    skeleton_mid,
    skeleton_low,
):
    rows, rank = panel_top.shape
    many = lax.axis_size("pts")
    leaf = lax.axis_index("leaf")
    core, plane = leaf % 2, leaf // 2
    device = leaf * many + lax.axis_index("pts")
    core_arg = core.astype(jnp.int32).reshape(1)
    panels = (panel_low, panel_mid, panel_top)
    zero2 = jnp.zeros((2, rank), F32)
    each = rank // (2 * many)

    keep, send = call_product(core_arg, (solved_low,), panels, many)
    first = exchanged(keep + swap(send, 1)).sum(axis=0)
    keep, send = call_product(core_arg, (solved_mid, solved_top, leaf_solved), panels, many)
    rest = keep + swap(send, 1)
    take = lambda table, k: lax.dynamic_index_in_dim(table, k, 0, keepdims=False)
    listed = jnp.concatenate(
        [take(skeleton_low, plane), take(skeleton_mid, plane // 2), take(skeleton_top, plane // 4)]
    )
    offsets = listed - device * rows
    select = (offsets[:, None] == jnp.arange(rows, dtype=jnp.int32)[None, :]).astype(F32)
    picked = jnp.einsum("cr,sr->cs", points, select, precision=BEST)
    pick_low, pick_mid, pick_top = (picked[:, k * rank : (k + 1) * rank] for k in range(3))

    mark = jnp.concatenate([pick_low, jnp.zeros((5, rank), F32)], 0)
    first_o = swap(jnp.concatenate([first[:, :rank], mark], 1), 2)
    spots = jnp.concatenate([pick_low, first_o[:3, rank:], zero2], 0)
    piece = jnp.concatenate([first, first_o[:, :rank], spots], 1)
    wide = piece.shape[1]
    got = exchanged(jnp.concatenate([to_all(piece), rest], 2))
    mine = got[:, :, :wide].reshape(-1, wide)
    theirs = swap(mine, 1)
    rest = got[:, :, wide:].sum(axis=0)
    own = jnp.concatenate([rest[:, 3 * k * rank : 3 * (k + 1) * rank] for k in range(3)], 0)
    other = swap(own[:, :rank], 2)
    low, mid = call_level(core_arg, mine, theirs, own, other, (0, rank, 2 * rank, 3 * rank, 4 * rank))

    marks = jnp.concatenate([pick_mid, pick_top, zero2], 0)
    mid = jnp.concatenate([mid, jnp.concatenate([marks, jnp.zeros_like(marks)], 1)], 0)
    mid = mid + swap(mid, 2)
    mid_o = swap(mid[:, :rank], 4)
    marks, marks_o = mid[3 * each :, :rank], mid_o[3 * each :]
    spots = jnp.concatenate([marks[:3], marks_o[:3], zero2], 0)
    marks = marks + marks_o
    mine = spread_to_all(jnp.concatenate([mid[:each], mid_o[:each], spots], 1))
    theirs = swap(mine, 1)
    ans, top = call_level(
        core_arg, mine, theirs, mid[each : 3 * each], mid_o[each : 3 * each], (0, rank, rank, 2 * rank, 3 * rank)
    )

    top = top + swap(top, 4)
    top_o = swap(jnp.concatenate([top, marks], 0), 8)
    spots = jnp.concatenate([marks[3:6], top_o[2 * each + 3 : 2 * each + 6], zero2], 0)
    blocks = [top[:each], top[each:], top_o[:each], top_o[each : 2 * each], spots]
    blocks += [ans[:each], ans[each:], low[:each], low[each : 2 * each], low[2 * each :]]
    mine = spread_to_all(jnp.concatenate(blocks, 1))
    theirs = swap(mine, 1)
    return call_top(core_arg, mine, theirs, (leaf_solved, solved_top, solved_mid, solved_low))


def solution(mesh):
    split = P(("leaf", "pts"), None)
    in_specs = (split, P(None, ("leaf", "pts")), *[split] * 6, P(), P(), P())

    return jax.shard_map(per_device, mesh=mesh, in_specs=in_specs, out_specs=split, check_vma=False)
```

profile of v0, /device:TPU:32, one launch (start us, length us, event | category | flops | bytes accessed | tf_op | source)
XLA Modules:
  0.0 147.5 jit_solution(11854354348314600968)
XLA Ops:
  0.0 8.3 %shard_map.110 = (f32[16,8,2304]{2,1,0:T(8,128)}, f32[16,8,2304]{2,1,0:T(8,128)}) custom-call(s32[1]{0:T(128)} %bitcast.core_ref, f32[1024,256]{1,0:T(8,128)} %refs_2_.5, f32[1024,256]{1,0:T(8,128)} %refs_1_.5, f32[1024,256]{1,0:T(8,128)} %refs_0_.5, f32[1024,256]{1,0:T(8,128)} %refs_3_.4, f32[1024,256]{1,0:T(8,128)} %refs_4_.1, f32[1024,256]{1,0:T(8,128)} %refs_5_.1), custom_call_target="tpu_custom_call" | custom-call | flops 3623878656 | bytes 6291456 | tf_op jit(solution)/shard_map/pallas_call | solution.py:73
  8.4 4.6 %shard_map.109 = (f32[16,8,768]{2,1,0:T(8,128)}, f32[16,8,768]{2,1,0:T(8,128)}) custom-call(s32[1]{0:T(128)} %bitcast.core_ref, f32[1024,256]{1,0:T(8,128)} %refs_3_.5, f32[1024,256]{1,0:T(8,128)} %refs_3_.4, f32[1024,256]{1,0:T(8,128)} %refs_4_.1, f32[1024,256]{1,0:T(8,128)} %refs_5_.1), custom_call_target="tpu_custom_call" | custom-call | flops 1207959552 | bytes 4194304 | tf_op jit(solution)/shard_map/pallas_call | solution.py:73
  14.3 0.7 constant_dynamic-slice_fusion.2
  15.2 1.8 %add.42 = f32[16,8,768]{2,1,0:T(8,128)} add(f32[16,8,768]{2,1,0:T(8,128)} %get-tuple-element.13, f32[16,8,768]{2,1,0:T(8,128)S(1)} %collective-permute-done) | non-fusion elementwise | flops 98304 | bytes 1179648 | tf_op jit(solution)/shard_map/add | solution.py:307
  16.9 7.0 %all-to-all-start = ((f32[16,8,768]{2,1,0:T(8,128)}), f32[16,8,768]{2,1,0:T(8,128)S(1)}, u32[]{:S(2)}, u32[]{:S(2)}) async-start(f32[16,8,768]{2,1,0:T(8,128)} %add.42), calls=%async_computation | async-start | bytes 786432 | tf_op jit(solution)/shard_map/all_to_all | solution.py:276
  24.0 1.5 %fusion.2 = f32[3,768]{1,0:T(4,128)S(1)} fusion(f32[3,1024]{1,0:T(4,128)S(1)} %copy-done, s32[768]{0:T(1024)S(1)} %add_subtract_fusion), kind=kOutput, calls=%fused_computation.5 | convolution fusion | flops 29097984 | bytes 24576 | tf_op jit(solution)/shard_map/cr,sr->cs/dot_general | solution.py:316
  25.5 8.8 %all-to-all-done = f32[16,8,768]{2,1,0:T(8,128)S(1)} async-done(((f32[16,8,768]{2,1,0:T(8,128)}), f32[16,8,768]{2,1,0:T(8,128)S(1)}, u32[]{:S(2)}, u32[]{:S(2)}) %all-to-all-start) | async-done | bytes 393248 | tf_op jit(solution)/shard_map/all_to_all | solution.py:276
  34.6 3.6 %collective-permute-done.1 = f32[8,512]{1,0:T(8,128)S(1)} collective-permute-done((f32[8,512]{1,0:T(8,128)S(1)}, f32[8,512]{1,0:T(8,128)S(1)}, u32[]{:S(2)}, u32[]{:S(2)}) %collective-permute-start.1) | collective-permute-done | bytes 16416 | tf_op jit(solution)/shard_map/ppermute | solution.py:268
  38.6 27.1 %all_to_all.20 = f32[16,8,3584]{2,1,0:T(8,128)S(1)} all-to-all(f32[16,8,3584]{2,1,0:T(8,128)S(1)} %pad_maximum_fusion), channel_id=1, replica_groups=mesh['leaf'=16,'pts'=16] {'pts'}, dimensions={0} | all-to-all | bytes 3670016 | tf_op jit(solution)/shard_map/all_to_all | solution.py:276
  66.6 3.5 %collective-permute-done.4.other_ref = f32[24,256]{1,0:T(8,128)S(1)} collective-permute-done((f32[24,256]{1,0:T(8,128)S(1)}, f32[24,256]{1,0:T(8,128)S(1)}, u32[]{:S(2)}, u32[]{:S(2)}) %collective-permute-start.4) | collective-permute-done | bytes 24608 | tf_op jit(solution)/shard_map/ppermute | solution.py:268
  70.1 3.9 %shard_map.111 = (f32[24,256]{1,0:T(8,128)S(1)}, f32[24,512]{1,0:T(8,128)S(1)}) custom-call(s32[1]{0:T(128)} %bitcast.core_ref, f32[128,1280]{1,0:T(8,128)S(1)} %slice_bitcast_fusion.mine_ref, f32[128,1280]{1,0:T(8,128)S(1)} %collective-permute-done.3.theirs_ref, f32[24,768]{1,0:T(8,128)S(1)} %pad_maximum_fusion.1.own_ref, ...), custom_call_target="tpu_custom_call" | custom-call | flops 2684354560 | bytes 1310720 | tf_op jit(solution)/shard_map/pallas_call | solution.py:193
  74.4 4.0 %collective-permute-done.5 = f32[32,512]{1,0:T(8,128)S(1)} collective-permute-done((f32[32,512]{1,0:T(8,128)S(1)}, f32[32,512]{1,0:T(8,128)S(1)}, u32[]{:S(2)}, u32[]{:S(2)}) %collective-permute-start.5) | collective-permute-done | bytes 65568 | tf_op jit(solution)/shard_map/ppermute | solution.py:268
  78.4 3.3 %collective-permute-start.6 = (f32[32,256]{1,0:T(8,128)S(1)}, f32[32,256]{1,0:T(8,128)S(1)}, u32[]{:S(2)}, u32[]{:S(2)}) collective-permute-start(f32[32,256]{1,0:T(8,128)S(1)} %slice.143), channel_id=1, source_target_pairs={{0,64},{16,80},{32,96},{48,112},{64,0},{80,16},{96,32},{112,48},{1... | collective-permute-start | bytes 98312 | tf_op jit(solution)/shard_map/ppermute | solution.py:268
  81.8 1.9 %collective-permute-done.6 = f32[32,256]{1,0:T(8,128)S(1)} collective-permute-done((f32[32,256]{1,0:T(8,128)S(1)}, f32[32,256]{1,0:T(8,128)S(1)}, u32[]{:S(2)}, u32[]{:S(2)}) %collective-permute-start.6) | collective-permute-done | bytes 32800 | tf_op jit(solution)/shard_map/ppermute | solution.py:268
  83.7 13.6 %all_to_all.21 = f32[16,8,1024]{2,1,0:T(8,128)S(1)} all-to-all(f32[16,8,1024]{2,1,0:T(8,128)S(1)} %broadcast_in_dim.18), channel_id=1, replica_groups=mesh['leaf'=16,'pts'=16] {'pts'}, dimensions={0} | all-to-all | bytes 1048576 | tf_op jit(solution)/shard_map/all_to_all | solution.py:276
  97.3 1.9 %collective-permute-done.7.theirs_ref = f32[128,1024]{1,0:T(8,128)S(1)} collective-permute-done((f32[128,1024]{1,0:T(8,128)S(1)}, f32[128,1024]{1,0:T(8,128)S(1)}, u32[]{:S(2)}, u32[]{:S(2)}) %collective-permute-start.7) | collective-permute-done | bytes 524320 | tf_op jit(solution)/shard_map/ppermute | solution.py:268
  99.2 4.0 %shard_map.112 = (f32[16,256]{1,0:T(8,128)S(1)}, f32[16,256]{1,0:T(8,128)S(1)}) custom-call(s32[1]{0:T(128)} %bitcast.core_ref, f32[128,1024]{1,0:T(8,128)S(1)} %bitcast.14, f32[128,1024]{1,0:T(8,128)S(1)} %collective-permute-done.7.theirs_ref, f32[16,512]{1,0:T(8,128)S(1)} %slice.147.own_ref, f32[16,256]{1,0:T(8,128)S(1)} %slice.148.other_ref), custom_call_target="tpu_custom_call" | custom-call | flops 2684354560 | bytes 1048576 | tf_op jit(solution)/shard_map/pallas_call | solution.py:193
  103.2 3.1 %collective-permute-start.8 = (f32[16,256]{1,0:T(8,128)S(1)}, f32[16,256]{1,0:T(8,128)S(1)}, u32[]{:S(2)}, u32[]{:S(2)}) collective-permute-start(f32[16,256]{1,0:T(8,128)S(1)} %get-tuple-element.18), channel_id=1, source_target_pairs={{0,64},{16,80},{32,96},{48,112},{64,0},{80,16},{96,32},{112,48},{1... | collective-permute-start | bytes 49160 | tf_op jit(solution)/shard_map/ppermute | solution.py:268
  106.3 1.7 %collective-permute-done.8 = f32[16,256]{1,0:T(8,128)S(1)} collective-permute-done((f32[16,256]{1,0:T(8,128)S(1)}, f32[16,256]{1,0:T(8,128)S(1)}, u32[]{:S(2)}, u32[]{:S(2)}) %collective-permute-start.8) | collective-permute-done | bytes 16416 | tf_op jit(solution)/shard_map/ppermute | solution.py:268
  108.0 5.9 %collective-permute-start.9 = (f32[24,256]{1,0:T(8,128)S(1)}, f32[24,256]{1,0:T(8,128)S(1)}, u32[]{:S(2)}, u32[]{:S(2)}) collective-permute-start(f32[24,256]{1,0:T(8,128)S(1)} %pad_maximum_fusion.2), channel_id=1, source_target_pairs={{0,128},{16,144},{32,160},{48,176},{64,192},{80,208},{96,224},{112... | collective-permute-start | bytes 73736 | tf_op jit(solution)/shard_map/ppermute | solution.py:268
  113.9 1.9 %collective-permute-done.9 = f32[24,256]{1,0:T(8,128)S(1)} collective-permute-done((f32[24,256]{1,0:T(8,128)S(1)}, f32[24,256]{1,0:T(8,128)S(1)}, u32[]{:S(2)}, u32[]{:S(2)}) %collective-permute-start.9) | collective-permute-done | bytes 24608 | tf_op jit(solution)/shard_map/ppermute | solution.py:268
  116.1 21.5 %all_to_all.22 = f32[16,8,2560]{2,1,0:T(8,128)S(1)} all-to-all(f32[16,8,2560]{2,1,0:T(8,128)S(1)} %broadcast_in_dim.19), channel_id=1, replica_groups=mesh['leaf'=16,'pts'=16] {'pts'}, dimensions={0} | all-to-all | bytes 2621440 | tf_op jit(solution)/shard_map/all_to_all | solution.py:276
  137.6 3.0 %collective-permute-done.10.theirs_ref = f32[128,2560]{1,0:T(8,128)S(1)} collective-permute-done((f32[128,2560]{1,0:T(8,128)S(1)}, f32[128,2560]{1,0:T(8,128)S(1)}, u32[]{:S(2)}, u32[]{:S(2)}) %collective-permute-start.10) | collective-permute-done | bytes 1310752 | tf_op jit(solution)/shard_map/ppermute | solution.py:268
  140.6 6.7 %shard_map.113 = f32[1024,256]{1,0:T(8,128)} custom-call(s32[1]{0:T(128)} %bitcast.core_ref, f32[128,2560]{1,0:T(8,128)S(1)} %bitcast.12, f32[128,2560]{1,0:T(8,128)S(1)} %collective-permute-done.10.theirs_ref, f32[1024,256]{1,0:T(8,128)S(1)} %copy-done.3, f32[1024,256]{1,0:T(8,128)S(1)} %copy-done.2, f32[1024,256]{1,0:T(8,128)S(1)} %copy-done.1, ...), custom_call_target="tpu_custom_call" | custom-call | flops 3355443200 | bytes 7864320 | tf_op jit(solution)/shard_map/pallas_call | solution.py:250
  (71 shorter events, 3.6 us)
Async XLA Ops:
  0.0 24.0 %copy-start = (f32[3,1024]{1,0:T(4,128)S(1)}, f32[3,1024]{1,0:T(4,128)}, u32[]{:S(2)}) copy-start(f32[3,1024]{1,0:T(4,128)} %param.12) | copy-start | bytes 36868
  8.3 5.3 %copy-start.6 = (s32[2,256]{1,0:T(2,128)S(1)}, s32[2,256]{1,0:T(2,128)}, u32[]{:S(2)}) copy-start(s32[2,256]{1,0:T(2,128)} %param.19) | copy-start | bytes 6148
  8.3 29.9 %collective-permute-start.2 = (f32[16,8,2304]{2,1,0:T(8,128)}, f32[16,8,2304]{2,1,0:T(8,128)S(1)}, u32[]{:S(2)}, u32[]{:S(2)}) collective-permute-start(f32[16,8,2304]{2,1,0:T(8,128)} %get-tuple-element.16), channel_id=1, source_target_pairs={{0,16},{16,0},{32,48},{48,32},{64,80},{80,64},{96,112},{112,96},{1... | collective-permute-start | bytes 3538952 | tf_op jit(solution)/shard_map/ppermute | solution.py:268
  13.0 25.2 %copy-start.5 = (f32[16,8,2304]{2,1,0:T(8,128)S(1)}, f32[16,8,2304]{2,1,0:T(8,128)}, u32[]{:S(2)}) copy-start(f32[16,8,2304]{2,1,0:T(8,128)} %get-tuple-element.15) | copy-start | bytes 3538948
  13.0 2.1 %collective-permute-start = (f32[16,8,768]{2,1,0:T(8,128)}, f32[16,8,768]{2,1,0:T(8,128)S(1)}, u32[]{:S(2)}, u32[]{:S(2)}) collective-permute-start(f32[16,8,768]{2,1,0:T(8,128)} %get-tuple-element.14), channel_id=1, source_target_pairs={{0,16},{16,0},{32,48},{48,32},{64,80},{80,64},{96,112},{112,96},{1... | collective-permute-start | bytes 1179656 | tf_op jit(solution)/shard_map/ppermute | solution.py:268
  16.9 17.4 %all-to-all-start = ((f32[16,8,768]{2,1,0:T(8,128)}), f32[16,8,768]{2,1,0:T(8,128)S(1)}, u32[]{:S(2)}, u32[]{:S(2)}) async-start(f32[16,8,768]{2,1,0:T(8,128)} %add.42), calls=%async_computation | async-start | bytes 786432 | tf_op jit(solution)/shard_map/all_to_all | solution.py:276
  34.4 3.8 %collective-permute-start.1 = (f32[8,512]{1,0:T(8,128)S(1)}, f32[8,512]{1,0:T(8,128)S(1)}, u32[]{:S(2)}, u32[]{:S(2)}) collective-permute-start(f32[8,512]{1,0:T(8,128)S(1)} %select_maximum_fusion.1), channel_id=1, source_target_pairs={{0,32},{16,48},{32,0},{48,16},{64,96},{80,112},{96,64},{112,80},{1... | collective-permute-start | bytes 49160 | tf_op jit(solution)/shard_map/ppermute | solution.py:268
  65.8 4.3 %collective-permute-start.3 = (f32[128,1280]{1,0:T(8,128)S(1)}, f32[128,1280]{1,0:T(8,128)S(1)}, u32[]{:S(2)}, u32[]{:S(2)}) collective-permute-start(f32[128,1280]{1,0:T(8,128)S(1)} %slice_bitcast_fusion.mine_ref), channel_id=1, source_target_pairs={{0,16},{16,0},{32,48},{48,32},{64,80},{80,64},{96,112},{112,96},{1... | collective-permute-start | bytes 1966088 | tf_op jit(solution)/shard_map/ppermute | solution.py:268
  66.0 4.1 %collective-permute-start.4 = (f32[24,256]{1,0:T(8,128)S(1)}, f32[24,256]{1,0:T(8,128)S(1)}, u32[]{:S(2)}, u32[]{:S(2)}) collective-permute-start(f32[24,256]{1,0:T(8,128)S(1)} %slice.139), channel_id=1, source_target_pairs={{0,32},{16,48},{32,0},{48,16},{64,96},{80,112},{96,64},{112,80},{1... | collective-permute-start | bytes 73736 | tf_op jit(solution)/shard_map/ppermute | solution.py:268
  74.0 4.4 %collective-permute-start.5 = (f32[32,512]{1,0:T(8,128)S(1)}, f32[32,512]{1,0:T(8,128)S(1)}, u32[]{:S(2)}, u32[]{:S(2)}) collective-permute-start(f32[32,512]{1,0:T(8,128)S(1)} %select_maximum_fusion), channel_id=1, source_target_pairs={{0,32},{16,48},{32,0},{48,16},{64,96},{80,112},{96,64},{112,80},{1... | collective-permute-start | bytes 196616 | tf_op jit(solution)/shard_map/ppermute | solution.py:268
  78.4 5.2 %collective-permute-start.6 = (f32[32,256]{1,0:T(8,128)S(1)}, f32[32,256]{1,0:T(8,128)S(1)}, u32[]{:S(2)}, u32[]{:S(2)}) collective-permute-start(f32[32,256]{1,0:T(8,128)S(1)} %slice.143), channel_id=1, source_target_pairs={{0,64},{16,80},{32,96},{48,112},{64,0},{80,16},{96,32},{112,48},{1... | collective-permute-start | bytes 98312 | tf_op jit(solution)/shard_map/ppermute | solution.py:268
  97.3 1.9 %collective-permute-start.7 = (f32[128,1024]{1,0:T(8,128)S(1)}, f32[128,1024]{1,0:T(8,128)S(1)}, u32[]{:S(2)}, u32[]{:S(2)}) collective-permute-start(f32[128,1024]{1,0:T(8,128)S(1)} %bitcast.13), channel_id=1, source_target_pairs={{0,16},{16,0},{32,48},{48,32},{64,80},{80,64},{96,112},{112,96},{1... | collective-permute-start | bytes 1572872 | tf_op jit(solution)/shard_map/ppermute | solution.py:268
  99.2 41.4 %copy-start.4 = (f32[1024,256]{1,0:T(8,128)S(1)}, f32[1024,256]{1,0:T(8,128)}, u32[]{:S(2)}) copy-start(f32[1024,256]{1,0:T(8,128)} %refs_3_.5) | copy-start | bytes 3145732
  103.2 4.8 %collective-permute-start.8 = (f32[16,256]{1,0:T(8,128)S(1)}, f32[16,256]{1,0:T(8,128)S(1)}, u32[]{:S(2)}, u32[]{:S(2)}) collective-permute-start(f32[16,256]{1,0:T(8,128)S(1)} %get-tuple-element.18), channel_id=1, source_target_pairs={{0,64},{16,80},{32,96},{48,112},{64,0},{80,16},{96,32},{112,48},{1... | collective-permute-start | bytes 49160 | tf_op jit(solution)/shard_map/ppermute | solution.py:268
  108.0 7.8 %collective-permute-start.9 = (f32[24,256]{1,0:T(8,128)S(1)}, f32[24,256]{1,0:T(8,128)S(1)}, u32[]{:S(2)}, u32[]{:S(2)}) collective-permute-start(f32[24,256]{1,0:T(8,128)S(1)} %pad_maximum_fusion.2), channel_id=1, source_target_pairs={{0,128},{16,144},{32,160},{48,176},{64,192},{80,208},{96,224},{112... | collective-permute-start | bytes 73736 | tf_op jit(solution)/shard_map/ppermute | solution.py:268
  115.9 24.7 %copy-start.1 = (f32[1024,256]{1,0:T(8,128)S(1)}, f32[1024,256]{1,0:T(8,128)}, u32[]{:S(2)}) copy-start(f32[1024,256]{1,0:T(8,128)} %refs_2_.5) | copy-start | bytes 3145732
  115.9 24.7 %copy-start.2 = (f32[1024,256]{1,0:T(8,128)S(1)}, f32[1024,256]{1,0:T(8,128)}, u32[]{:S(2)}) copy-start(f32[1024,256]{1,0:T(8,128)} %refs_1_.5) | copy-start | bytes 3145732
  115.9 24.7 %copy-start.3 = (f32[1024,256]{1,0:T(8,128)S(1)}, f32[1024,256]{1,0:T(8,128)}, u32[]{:S(2)}) copy-start(f32[1024,256]{1,0:T(8,128)} %refs_0_.5) | copy-start | bytes 3145732
  137.6 3.0 %collective-permute-start.10 = (f32[128,2560]{1,0:T(8,128)S(1)}, f32[128,2560]{1,0:T(8,128)S(1)}, u32[]{:S(2)}, u32[]{:S(2)}) collective-permute-start(f32[128,2560]{1,0:T(8,128)S(1)} %bitcast.11), channel_id=1, source_target_pairs={{0,16},{16,0},{32,48},{48,32},{64,80},{80,64},{96,112},{112,96},{1... | collective-permute-start | bytes 3932168 | tf_op jit(solution)/shard_map/ppermute | solution.py:268
where the time goes:
time: 150 us; the launch traced here: 148 us
  blocking collectives  62.2 us (41%)
  waiting for transfers between devices  30.5 us (20%)
  Pallas kernels  27.5 us (18%)
  starting transfers between devices  21.3 us (14%)
  other arithmetic  2.27 us (2%)
  local copies, waits for them, and re-layouts  1.76 us (1%)
  matrix products  1.54 us (1%)
    all_to_all x3, blocking collectives, exchanged(): return lax.all_to_all(pieces, 'pts', 0, 0, tiled=True)  62.2 us
    ppermute x11, waiting for transfers between devices, swap(): return lax.ppermute(value, 'leaf', [(i, i ^ mask) for i in range(count)])  21.7 us
    ppermute x11, starting transfers between devices, swap(): return lax.ppermute(value, 'leaf', [(i, i ^ mask) for i in range(count)])  14.2 us
    pallas_call x2, Pallas kernels, call_product(): pl.pallas_call(functools.partial(product_kernel, count), out_shape=(half,...  12.9 us
    all_to_all x1, waiting for transfers between devices, exchanged(): return lax.all_to_all(pieces, 'pts', 0, 0, tiled=True)  8.8 us
    pallas_call x2, Pallas kernels, call_level(): pl.pallas_call(functools.partial(level_kernel, at), out_shape=(jax.ShapeD...  7.86 us
    all_to_all x1, starting transfers between devices, exchanged(): return lax.all_to_all(pieces, 'pts', 0, 0, tiled=True)  7.03 us
    pallas_call x1, Pallas kernels, call_top(): pl.pallas_call(top_kernel, out_shape=jax.ShapeDtypeStruct((rows, rank), F...  6.73 us
  transfers between devices with their start and end apart: 12, of which 10 were waited for; matrix products, arithmetic and copies ran while one was open for 3% of the time, Pallas kernels for 3%

commit v1 on v0

--- a/solution.py
+++ b/solution.py
@@ -27,13 +27,17 @@
 
 def mm3(a, b, by=dot):
     (a1, a2), (b1, b2) = a, b
-    return by(a1, b1) + (by(a1, b2) + by(a2, b1))
+    rows = a1.shape[0]
+    if rows % 128:
+        return by(a1, b1) + (by(a1, b2) + by(a2, b1))
+    both = by(jnp.concatenate([a1, a2], 0), b1)
+    return both[:rows] + (both[rows:] + by(a1, b2))
 
 
 def product_kernel(count, core_ref, *refs):
     sources = refs[: count + 3]
-    keep_ref, send_ref, acc, side1, side2, piece1, piece2, come = refs[count + 3 : count + 11]
-    held = refs[count + 11 :]
+    keep_ref, send_ref, acc, come = refs[count + 3 : count + 7]
+    held = refs[count + 7 :]
     rows, rank = held[0].shape
     chunk = rank
     loads = []
@@ -47,16 +51,12 @@
         at = slice(i * chunk, (i + 1) * chunk)
         for load in loads[i * (count + 3) : (i + 1) * (count + 3)]:
             load.wait()
-        for b in range(count):
-            band = slice(b * rank, (b + 1) * rank)
-            side1[band, at], side2[band, at] = cut(jnp.transpose(held[b][at, :]))
+        sides = [cut(jnp.transpose(held[b][at, :])) for b in range(count)]
+        side = tuple(jnp.concatenate(part, 0) for part in zip(*sides))
         for k in range(3):
             band = slice(k * rank, (k + 1) * rank)
-            piece1[at, band], piece2[at, band] = cut(held[count + k][at, :])
-    for k in range(3):
-        band = slice(k * rank, (k + 1) * rank)
-        one, two = piece1[:, band], piece2[:, band]
-        acc[:, band] = dot(side1[...], one) + (dot(side1[...], two) + dot(side2[...], one))
+            term = mm3(side, cut(held[count + k][at, :]))
+            acc[:, band] = term if i == 0 else acc[:, band] + term
     core = core_ref[0]
     for ref, which in ((keep_ref, core), (send_ref, 1 - core)):
         for p in range(keep_ref.shape[0]):
@@ -76,14 +76,12 @@
         in_specs=[pl.BlockSpec(memory_space=pltpu.SMEM)] + [pl.BlockSpec(memory_space=pltpu.HBM)] * (count + 3),
         out_specs=(vm, vm),
         scratch_shapes=[pltpu.VMEM((count * rank, 3 * rank), F32)]
-        + [pltpu.VMEM((count * rank, rows), jnp.bfloat16)] * 2
-        + [pltpu.VMEM((rows, 3 * rank), jnp.bfloat16)] * 2
         + [pltpu.SemaphoreType.DMA((rows // rank, count + 3))]
         + [pltpu.VMEM((rows, rank), F32)] * (count + 3),
         cost_estimate=pl.CostEstimate(
             flops=count * 18 * rows * rank * rank, bytes_accessed=4 * rows * rank * (count + 3), transcendentals=0
         ),
-        compiler_params=pltpu.CompilerParams(vmem_limit_bytes=60 * 1024 * 1024),
+        compiler_params=pltpu.CompilerParams(vmem_limit_bytes=52 * 1024 * 1024),
     )(core, *columns, *panels)
 
 
@@ -99,13 +97,12 @@
     y_ref[...] = ident + n_ref[...]
     e_ref[...] = n_ref[...]
 
-    @pl.loop(0, 2)
-    def _(step):
-        before = cut(e_ref[...])
-        square = mm3(before, before)
+    for _ in range(2):
+        some = e_ref[...].astype(jnp.bfloat16)
+        square = dot(some, some)
         e_ref[...] = square
         y = y_ref[...]
-        y_ref[...] = y + mm3(cut(y), cut(square))
+        y_ref[...] = y + dot(y.astype(jnp.bfloat16), square.astype(jnp.bfloat16))
 
     def residual():
         y = y_ref[...]
@@ -184,6 +181,65 @@
     ans = mm3(cut(target), cut(y[...]))
     ans_ref[...] = ans
     next_ref[...] = own_ref[:, rank : rank + upper] - mm3(cut(ans), cut(full[:, upper_at : upper_at + upper]))
+
+
+def solve_kernel(at, core_ref, mine_ref, theirs_ref, couple_ref, far_ref, y_ref, up_ref, full, n, e):
+    rank = full.shape[0]
+    gram_at, upper_at, upper, gram_o_at, spot_at = at
+    place(core_ref, mine_ref, theirs_ref, full)
+    couple = couple_of(spots_of(mine_ref, theirs_ref, spot_at))
+    far = mm3(cut(full[:, gram_o_at : gram_o_at + rank]), cut(jnp.transpose(couple)))
+    n[...] = mm3(cut(mm3(cut(full[:, gram_at : gram_at + rank]), cut(couple))), cut(far))
+    couple_ref[...] = couple
+    far_ref[...] = far
+    up_ref[...] = full[:, upper_at : upper_at + upper]
+    inverse_into(n, y_ref, e)
+
+
+def call_solve(core, mine, theirs, at):
+    rank, upper = 2 * mine.shape[0], at[2]
+    vm = pl.BlockSpec(memory_space=pltpu.VMEM)
+    square = jax.ShapeDtypeStruct((rank, rank), F32)
+    return pl.pallas_call(
+        functools.partial(solve_kernel, at),
+        out_shape=(square, square, square, jax.ShapeDtypeStruct((rank, upper), F32)),
+        in_specs=[pl.BlockSpec(memory_space=pltpu.SMEM), vm, vm],
+        out_specs=(vm, vm, vm, vm),
+        scratch_shapes=[pltpu.VMEM((rank, mine.shape[1]), F32)] + [pltpu.VMEM((rank, rank), F32)] * 2,
+        cost_estimate=pl.CostEstimate(
+            flops=60 * 2 * rank**3, bytes_accessed=4 * rank * mine.shape[1], transcendentals=rank * rank
+        ),
+        compiler_params=pltpu.CompilerParams(vmem_limit_bytes=16 * 1024 * 1024),
+    )(core, mine, theirs)
+
+
+def apply_kernel(couple_ref, far_ref, y_ref, up_ref, own_ref, other_ref, ans_ref, next_ref):
+    rank = couple_ref.shape[0]
+    couple = couple_ref[...]
+    near = mm3(cut(own_ref[:, :rank]), cut(couple))
+    target = mm3(cut(other_ref[...]), cut(couple), dot_t) - mm3(cut(near), cut(far_ref[...]))
+    ans = mm3(cut(target), cut(y_ref[...]))
+    ans_ref[...] = ans
+    next_ref[...] = own_ref[:, rank:] - mm3(cut(ans), cut(up_ref[...]))
+
+
+def call_apply(solved, own, other):
+    rank, upper = solved[3].shape
+    rows = own.shape[0]
+    vm = pl.BlockSpec(memory_space=pltpu.VMEM)
+    return pl.pallas_call(
+        apply_kernel,
+        out_shape=(
+            jax.ShapeDtypeStruct((rows, rank), F32),
+            jax.ShapeDtypeStruct((rows, upper), F32),
+        ),
+        in_specs=[vm] * 6,
+        out_specs=(vm, vm),
+        cost_estimate=pl.CostEstimate(
+            flops=30 * 2 * rows * rank**2, bytes_accessed=4 * rank * (3 * rank + upper), transcendentals=0
+        ),
+        compiler_params=pltpu.CompilerParams(vmem_limit_bytes=16 * 1024 * 1024),
+    )(*solved, own, other)
 
 
 def call_level(core, mine, theirs, own, other, at):
@@ -230,10 +286,9 @@
     stores = []
     for i in range(4):
         at = slice(i * chunk, (i + 1) * chunk)
-        total = held[0][at, :]
-        for k in range(3):
-            lanes = slice(k * rank, (k + 1) * rank)
-            total = total - mm3(cut(held[1 + k][at, :]), (stacked[0, :, lanes], stacked[1, :, lanes]), dot_t)
+        sides = [cut(held[1 + k][at, :]) for k in range(3)]
+        side = tuple(jnp.concatenate(part, 1) for part in zip(*sides))
+        total = held[0][at, :] - mm3(side, (stacked[0], stacked[1]), dot_t)
         result[at, :] = total
         store = pltpu.make_async_copy(result.at[at, :], out_ref.at[at, :], go.at[i])
         store.start()
@@ -303,9 +358,10 @@
     zero2 = jnp.zeros((2, rank), F32)
     each = rank // (2 * many)
 
-    keep, send = call_product(core_arg, (solved_low,), panels, many)
-    first = exchanged(keep + swap(send, 1)).sum(axis=0)
-    keep, send = call_product(core_arg, (solved_mid, solved_top, leaf_solved), panels, many)
+    keep, send = call_product(core_arg, (solved_low, solved_mid), panels, many)
+    both = exchanged(keep + swap(send, 1)).sum(axis=0)
+    first, middle = both[:, : 3 * rank], both[:, 3 * rank :]
+    keep, send = call_product(core_arg, (solved_top, leaf_solved), panels, many)
     rest = keep + swap(send, 1)
     take = lambda table, k: lax.dynamic_index_in_dim(table, k, 0, keepdims=False)
     listed = jnp.concatenate(
@@ -325,9 +381,10 @@
     mine = got[:, :, :wide].reshape(-1, wide)
     theirs = swap(mine, 1)
     rest = got[:, :, wide:].sum(axis=0)
-    own = jnp.concatenate([rest[:, 3 * k * rank : 3 * (k + 1) * rank] for k in range(3)], 0)
+    own = jnp.concatenate([middle, rest[:, : 3 * rank], rest[:, 3 * rank :]], 0)
     other = swap(own[:, :rank], 2)
-    low, mid = call_level(core_arg, mine, theirs, own, other, (0, rank, 2 * rank, 3 * rank, 4 * rank))
+    solved = call_solve(core_arg, mine, theirs, (0, rank, 2 * rank, 3 * rank, 4 * rank))
+    low, mid = call_apply(solved, own, other)
 
     marks = jnp.concatenate([pick_mid, pick_top, zero2], 0)
     mid = jnp.concatenate([mid, jnp.concatenate([marks, jnp.zeros_like(marks)], 1)], 0)
@@ -342,10 +399,10 @@
         core_arg, mine, theirs, mid[each : 3 * each], mid_o[each : 3 * each], (0, rank, rank, 2 * rank, 3 * rank)
     )
 
-    top = top + swap(top, 4)
-    top_o = swap(jnp.concatenate([top, marks], 0), 8)
-    spots = jnp.concatenate([marks[3:6], top_o[2 * each + 3 : 2 * each + 6], zero2], 0)
-    blocks = [top[:each], top[each:], top_o[:each], top_o[each : 2 * each], spots]
+    far1, far2 = swap(jnp.concatenate([top, marks], 0), 8), swap(top, 12)
+    top, top_o = top + swap(top, 4), far1[: 2 * each] + far2
+    spots = jnp.concatenate([marks[3:6], far1[2 * each + 3 : 2 * each + 6], zero2], 0)
+    blocks = [top[:each], top[each:], top_o[:each], top_o[each:], spots]
     blocks += [ans[:each], ans[each:], low[:each], low[each : 2 * each], low[2 * each :]]
     mine = spread_to_all(jnp.concatenate(blocks, 1))
     theirs = swap(mine, 1)

time: 150 us -> 144 us (0.960)
  blocking collectives: 62.2 us -> 57.6 us
  Pallas kernels: 27.5 us -> 23.6 us
  waiting for transfers between devices: 30.5 us -> 33.5 us
  starting transfers between devices: 21.3 us -> 19.5 us
    pallas_call x2 -> x1, Pallas kernels: 7.86 us -> 3.19 us  [call_level(): pl.pallas_call(functools.partial(level_kernel, at), out_shape=(jax.ShapeD...]
    all_to_all x3, blocking collectives: 62.2 us -> 57.6 us  [exchanged(): return lax.all_to_all(pieces, 'pts', 0, 0, tiled=True)]
    pallas_call x0 -> x2, Pallas kernels: none -> 3.6 us  [the longest x1 2.71 us: call_solve(): pl.pallas_call(functools.partial(solve_kernel, at), out_shape=(square, sq...]
    pallas_call x2, Pallas kernels: 12.9 us -> 10.9 us  [call_product(): pl.pallas_call(functools.partial(product_kernel, count), out_shape=(half,...]
    all_to_all x1, waiting for transfers between devices: 8.8 us -> 10.6 us  [exchanged(): return lax.all_to_all(pieces, 'pts', 0, 0, tiled=True)]
    ppermute x11 -> x12, starting transfers between devices: 14.2 us -> 12.5 us  [swap(): return lax.ppermute(value, 'leaf', [(i, i ^ mask) for i in range(count)])]
    ppermute x11 -> x12, waiting for transfers between devices: 21.7 us -> 22.8 us  [swap(): return lax.ppermute(value, 'leaf', [(i, i ^ mask) for i in range(count)])]
  transfers between devices with their start and end apart: 12 -> 13, of which waited for: 10 -> 9; matrix products, arithmetic and copies ran while one was open for 3% -> 5% of each run, Pallas kernels for 3% -> 6%
where the time goes in v1:
time: 144 us; the launch traced here: 142 us
  blocking collectives  57.6 us (40%)
  waiting for transfers between devices  33.5 us (23%)
  Pallas kernels  23.6 us (16%)
  starting transfers between devices  19.5 us (14%)
  other arithmetic  3.62 us (3%)
  local copies, waits for them, and re-layouts  1.77 us (1%)
  matrix products  1.54 us (1%)
    all_to_all x3, blocking collectives, exchanged(): return lax.all_to_all(pieces, 'pts', 0, 0, tiled=True)  57.6 us
    ppermute x12, waiting for transfers between devices, swap(): return lax.ppermute(value, 'leaf', [(i, i ^ mask) for i in range(count)])  22.8 us
    ppermute x12, starting transfers between devices, swap(): return lax.ppermute(value, 'leaf', [(i, i ^ mask) for i in range(count)])  12.5 us
    pallas_call x2, Pallas kernels, call_product(): pl.pallas_call(functools.partial(product_kernel, count), out_shape=(half,...  10.9 us
    all_to_all x1, waiting for transfers between devices, exchanged(): return lax.all_to_all(pieces, 'pts', 0, 0, tiled=True)  10.6 us
    all_to_all x1, starting transfers between devices, exchanged(): return lax.all_to_all(pieces, 'pts', 0, 0, tiled=True)  7.03 us
    pallas_call x1, Pallas kernels, call_top(): pl.pallas_call(top_kernel, out_shape=jax.ShapeDtypeStruct((rows, rank), F...  5.93 us
    pallas_call x1, Pallas kernels, call_level(): pl.pallas_call(functools.partial(level_kernel, at), out_shape=(jax.ShapeD...  3.19 us
  transfers between devices with their start and end apart: 13, of which 9 were waited for; matrix products, arithmetic and copies ran while one was open for 5% of the time, Pallas kernels for 6%

profile of v1, /device:TPU:32, one launch (start us, length us, event | category | flops | bytes accessed | tf_op | source)
XLA Modules:
  0.0 141.6 jit_solution(15952598042365079022)
XLA Ops:
  0.0 5.4 %shard_map.109 = (f32[16,8,1536]{2,1,0:T(8,128)S(1)}, f32[16,8,1536]{2,1,0:T(8,128)S(1)}) custom-call(s32[1]{0:T(128)} %bitcast.core_ref, f32[1024,256]{1,0:T(8,128)} %refs_3_.5, f32[1024,256]{1,0:T(8,128)} %refs_2_.5, f32[1024,256]{1,0:T(8,128)} %refs_2_.4, f32[1024,256]{1,0:T(8,128)} %refs_3_.4, f32[1024,256]{1,0:T(8,128)} %refs_4_.3), custom_call_target="tpu_custom_call" | custom-call | flops 2415919104 | bytes 5242880 | tf_op jit(solution)/shard_map/pallas_call | solution.py:73
  5.6 5.4 %shard_map.110 = (f32[16,8,1536]{2,1,0:T(8,128)S(1)}, f32[16,8,1536]{2,1,0:T(8,128)S(1)}) custom-call(s32[1]{0:T(128)} %bitcast.core_ref, f32[1024,256]{1,0:T(8,128)} %refs_1_.5, f32[1024,256]{1,0:T(8,128)} %refs_0_.5, f32[1024,256]{1,0:T(8,128)} %refs_2_.4, f32[1024,256]{1,0:T(8,128)} %refs_3_.4, f32[1024,256]{1,0:T(8,128)} %refs_4_.3), custom_call_target="tpu_custom_call" | custom-call | flops 2415919104 | bytes 5242880 | tf_op jit(solution)/shard_map/pallas_call | solution.py:73
  11.6 2.1 %add.45 = f32[16,8,1536]{2,1,0:T(8,128)} add(f32[16,8,1536]{2,1,0:T(8,128)S(1)} %get-tuple-element.17, f32[16,8,1536]{2,1,0:T(8,128)} %collective-permute-done) | non-fusion elementwise | flops 196608 | bytes 2359296 | tf_op jit(solution)/shard_map/add | solution.py:362
  13.7 7.0 %all-to-all-start = ((f32[16,8,1536]{2,1,0:T(8,128)}), f32[16,8,1536]{2,1,0:T(8,128)S(1)}, u32[]{:S(2)}, u32[]{:S(2)}) async-start(f32[16,8,1536]{2,1,0:T(8,128)} %add.45), calls=%async_computation | async-start | bytes 1572864 | tf_op jit(solution)/shard_map/all_to_all | solution.py:331
  22.2 1.5 %fusion.2 = f32[3,768]{1,0:T(4,128)S(1)} fusion(f32[3,1024]{1,0:T(4,128)S(1)} %copy-done, s32[768]{0:T(1024)S(1)} %add_subtract_fusion), kind=kOutput, calls=%fused_computation.4 | convolution fusion | flops 29097984 | bytes 24576 | tf_op jit(solution)/shard_map/cr,sr->cs/dot_general | solution.py:372
  23.7 1.2 add.50
  25.0 10.6 %all-to-all-done = f32[16,8,1536]{2,1,0:T(8,128)S(1)} async-done(((f32[16,8,1536]{2,1,0:T(8,128)}), f32[16,8,1536]{2,1,0:T(8,128)S(1)}, u32[]{:S(2)}, u32[]{:S(2)}) %all-to-all-start) | async-done | bytes 786464 | tf_op jit(solution)/shard_map/all_to_all | solution.py:331
  35.9 3.6 %collective-permute-done.1 = f32[8,512]{1,0:T(8,128)S(1)} collective-permute-done((f32[8,512]{1,0:T(8,128)S(1)}, f32[8,512]{1,0:T(8,128)S(1)}, u32[]{:S(2)}, u32[]{:S(2)}) %collective-permute-start.1) | collective-permute-done | bytes 16416 | tf_op jit(solution)/shard_map/ppermute | solution.py:323
  39.7 22.1 %all_to_all.20 = f32[16,8,2816]{2,1,0:T(8,128)S(1)} all-to-all(f32[16,8,2816]{2,1,0:T(8,128)S(1)} %pad_maximum_fusion), channel_id=1, replica_groups=mesh['leaf'=16,'pts'=16] {'pts'}, dimensions={0} | all-to-all | bytes 2883584 | tf_op jit(solution)/shard_map/all_to_all | solution.py:331
  62.4 1.6 %collective-permute-done.3.theirs_ref = f32[128,1280]{1,0:T(8,128)S(1)} collective-permute-done((f32[128,1280]{1,0:T(8,128)S(1)}, f32[128,1280]{1,0:T(8,128)S(1)}, u32[]{:S(2)}, u32[]{:S(2)}) %collective-permute-start.3) | collective-permute-done | bytes 655392 | tf_op jit(solution)/shard_map/ppermute | solution.py:323
  64.0 2.7 %shard_map.111 = (f32[256,256]{1,0:T(8,128)S(1)}, f32[256,256]{1,0:T(8,128)S(1)}, f32[256,256]{1,0:T(8,128)S(1)}, f32[256,512]{1,0:T(8,128)S(1)}) custom-call(s32[1]{0:T(128)} %bitcast.core_ref, f32[128,1280]{1,0:T(8,128)S(1)} %slice_bitcast_fusion.mine_ref, f32[128,1280]{1,0:T(8,128)S(1)} %collective-permute-done.3.theirs_ref), custom_call_target="tpu_custom_call" | custom-call | flops 2013265920 | bytes 1310720 | tf_op jit(solution)/shard_map/pallas_call | solution.py:203
  68.0 4.0 %collective-permute-done.5 = f32[32,512]{1,0:T(8,128)S(1)} collective-permute-done((f32[32,512]{1,0:T(8,128)S(1)}, f32[32,512]{1,0:T(8,128)S(1)}, u32[]{:S(2)}, u32[]{:S(2)}) %collective-permute-start.5) | collective-permute-done | bytes 65568 | tf_op jit(solution)/shard_map/ppermute | solution.py:323
  72.0 3.4 %collective-permute-start.6 = (f32[32,256]{1,0:T(8,128)S(1)}, f32[32,256]{1,0:T(8,128)S(1)}, u32[]{:S(2)}, u32[]{:S(2)}) collective-permute-start(f32[32,256]{1,0:T(8,128)S(1)} %slice.153), channel_id=1, source_target_pairs={{0,64},{16,80},{32,96},{48,112},{64,0},{80,16},{96,32},{112,48},{1... | collective-permute-start | bytes 98312 | tf_op jit(solution)/shard_map/ppermute | solution.py:323
  75.4 1.9 %collective-permute-done.6 = f32[32,256]{1,0:T(8,128)S(1)} collective-permute-done((f32[32,256]{1,0:T(8,128)S(1)}, f32[32,256]{1,0:T(8,128)S(1)}, u32[]{:S(2)}, u32[]{:S(2)}) %collective-permute-start.6) | collective-permute-done | bytes 32800 | tf_op jit(solution)/shard_map/ppermute | solution.py:323
  77.4 13.6 %all_to_all.21 = f32[16,8,1024]{2,1,0:T(8,128)S(1)} all-to-all(f32[16,8,1024]{2,1,0:T(8,128)S(1)} %broadcast_in_dim.18), channel_id=1, replica_groups=mesh['leaf'=16,'pts'=16] {'pts'}, dimensions={0} | all-to-all | bytes 1048576 | tf_op jit(solution)/shard_map/all_to_all | solution.py:331
  91.0 1.9 %collective-permute-done.7.theirs_ref = f32[128,1024]{1,0:T(8,128)S(1)} collective-permute-done((f32[128,1024]{1,0:T(8,128)S(1)}, f32[128,1024]{1,0:T(8,128)S(1)}, u32[]{:S(2)}, u32[]{:S(2)}) %collective-permute-start.7) | collective-permute-done | bytes 524320 | tf_op jit(solution)/shard_map/ppermute | solution.py:323
  92.9 3.2 %shard_map.113 = (f32[16,256]{1,0:T(8,128)S(1)}, f32[16,256]{1,0:T(8,128)S(1)}) custom-call(s32[1]{0:T(128)} %bitcast.core_ref, f32[128,1024]{1,0:T(8,128)S(1)} %bitcast.14, f32[128,1024]{1,0:T(8,128)S(1)} %collective-permute-done.7.theirs_ref, f32[16,512]{1,0:T(8,128)S(1)} %slice.157.own_ref, f32[16,256]{1,0:T(8,128)S(1)} %slice.158.other_ref), custom_call_target="tpu_custom_call" | custom-call | flops 2684354560 | bytes 1048576 | tf_op jit(solution)/shard_map/pallas_call | solution.py:249
  96.1 3.0 %collective-permute-start.8 = (f32[16,256]{1,0:T(8,128)S(1)}, f32[16,256]{1,0:T(8,128)S(1)}, u32[]{:S(2)}, u32[]{:S(2)}) collective-permute-start(f32[16,256]{1,0:T(8,128)S(1)} %get-tuple-element.26), channel_id=1, source_target_pairs={{0,64},{16,80},{32,96},{48,112},{64,0},{80,16},{96,32},{112,48},{1... | collective-permute-start | bytes 49160 | tf_op jit(solution)/shard_map/ppermute | solution.py:323
  99.1 3.5 %collective-permute-start.10 = (f32[16,256]{1,0:T(8,128)S(1)}, f32[16,256]{1,0:T(8,128)S(1)}, u32[]{:S(2)}, u32[]{:S(2)}) collective-permute-start(f32[16,256]{1,0:T(8,128)S(1)} %get-tuple-element.26), channel_id=1, source_target_pairs={{0,192},{16,208},{32,224},{48,240},{64,128},{80,144},{96,160},{112... | collective-permute-start | bytes 49160 | tf_op jit(solution)/shard_map/ppermute | solution.py:323
  103.5 1.4 collective-permute-done.10
  104.9 5.4 %collective-permute-done.9 = f32[24,256]{1,0:T(8,128)S(1)} collective-permute-done((f32[24,256]{1,0:T(8,128)S(1)}, f32[24,256]{1,0:T(8,128)S(1)}, u32[]{:S(2)}, u32[]{:S(2)}) %collective-permute-start.9) | collective-permute-done | bytes 24608 | tf_op jit(solution)/shard_map/ppermute | solution.py:323
  110.6 21.8 %all_to_all.22 = f32[16,8,2560]{2,1,0:T(8,128)S(1)} all-to-all(f32[16,8,2560]{2,1,0:T(8,128)S(1)} %broadcast_in_dim.19), channel_id=1, replica_groups=mesh['leaf'=16,'pts'=16] {'pts'}, dimensions={0} | all-to-all | bytes 2621440 | tf_op jit(solution)/shard_map/all_to_all | solution.py:331
  132.4 3.0 %collective-permute-done.11.theirs_ref = f32[128,2560]{1,0:T(8,128)S(1)} collective-permute-done((f32[128,2560]{1,0:T(8,128)S(1)}, f32[128,2560]{1,0:T(8,128)S(1)}, u32[]{:S(2)}, u32[]{:S(2)}) %collective-permute-start.11) | collective-permute-done | bytes 1310752 | tf_op jit(solution)/shard_map/ppermute | solution.py:323
  135.5 5.9 %shard_map.114 = f32[1024,256]{1,0:T(8,128)} custom-call(s32[1]{0:T(128)} %bitcast.core_ref, f32[128,2560]{1,0:T(8,128)S(1)} %bitcast.12, f32[128,2560]{1,0:T(8,128)S(1)} %collective-permute-done.11.theirs_ref, f32[1024,256]{1,0:T(8,128)S(1)} %copy-done.2, f32[1024,256]{1,0:T(8,128)S(1)} %copy-done.1, f32[1024,256]{1,0:T(8,128)S(1)} %copy-done.4, ...), custom_call_target="tpu_custom_call" | custom-call | flops 3355443200 | bytes 7864320 | tf_op jit(solution)/shard_map/pallas_call | solution.py:305
  (74 shorter events, 5.6 us)
Async XLA Ops:
  0.0 22.2 %copy-start = (f32[3,1024]{1,0:T(4,128)S(1)}, f32[3,1024]{1,0:T(4,128)}, u32[]{:S(2)}) copy-start(f32[3,1024]{1,0:T(4,128)} %param.12) | copy-start | bytes 36868
  5.5 6.1 %copy-start.5 = (s32[2,256]{1,0:T(2,128)S(1)}, s32[2,256]{1,0:T(2,128)}, u32[]{:S(2)}) copy-start(s32[2,256]{1,0:T(2,128)} %param.19) | copy-start | bytes 6148
  5.5 6.1 %collective-permute-start = (f32[16,8,1536]{2,1,0:T(8,128)S(1)}, f32[16,8,1536]{2,1,0:T(8,128)}, u32[]{:S(2)}, u32[]{:S(2)}) collective-permute-start(f32[16,8,1536]{2,1,0:T(8,128)S(1)} %get-tuple-element.18), channel_id=1, source_target_pairs={{0,16},{16,0},{32,48},{48,32},{64,80},{80,64},{96,112},{112,96},{1... | collective-permute-start | bytes 2359304 | tf_op jit(solution)/shard_map/ppermute | solution.py:323
  11.0 12.7 %collective-permute-start.2 = (f32[16,8,1536]{2,1,0:T(8,128)S(1)}, f32[16,8,1536]{2,1,0:T(8,128)}, u32[]{:S(2)}, u32[]{:S(2)}) collective-permute-start(f32[16,8,1536]{2,1,0:T(8,128)S(1)} %get-tuple-element.20), channel_id=1, source_target_pairs={{0,16},{16,0},{32,48},{48,32},{64,80},{80,64},{96,112},{112,96},{1... | collective-permute-start | bytes 2359304 | tf_op jit(solution)/shard_map/ppermute | solution.py:323
  13.7 21.9 %all-to-all-start = ((f32[16,8,1536]{2,1,0:T(8,128)}), f32[16,8,1536]{2,1,0:T(8,128)S(1)}, u32[]{:S(2)}, u32[]{:S(2)}) async-start(f32[16,8,1536]{2,1,0:T(8,128)} %add.45), calls=%async_computation | async-start | bytes 1572864 | tf_op jit(solution)/shard_map/all_to_all | solution.py:331
  35.7 3.8 %collective-permute-start.1 = (f32[8,512]{1,0:T(8,128)S(1)}, f32[8,512]{1,0:T(8,128)S(1)}, u32[]{:S(2)}, u32[]{:S(2)}) collective-permute-start(f32[8,512]{1,0:T(8,128)S(1)} %select_maximum_fusion.1), channel_id=1, source_target_pairs={{0,32},{16,48},{32,0},{48,16},{64,96},{80,112},{96,64},{112,80},{1... | collective-permute-start | bytes 49160 | tf_op jit(solution)/shard_map/ppermute | solution.py:323
  61.8 2.2 %collective-permute-start.3 = (f32[128,1280]{1,0:T(8,128)S(1)}, f32[128,1280]{1,0:T(8,128)S(1)}, u32[]{:S(2)}, u32[]{:S(2)}) collective-permute-start(f32[128,1280]{1,0:T(8,128)S(1)} %slice_bitcast_fusion.mine_ref), channel_id=1, source_target_pairs={{0,16},{16,0},{32,48},{48,32},{64,80},{80,64},{96,112},{112,96},{1... | collective-permute-start | bytes 1966088 | tf_op jit(solution)/shard_map/ppermute | solution.py:323
  62.0 4.7 %collective-permute-start.4 = (f32[24,256]{1,0:T(8,128)S(1)}, f32[24,256]{1,0:T(8,128)S(1)}, u32[]{:S(2)}, u32[]{:S(2)}) collective-permute-start(f32[24,256]{1,0:T(8,128)S(1)} %slice.149), channel_id=1, source_target_pairs={{0,32},{16,48},{32,0},{48,16},{64,96},{80,112},{96,64},{112,80},{1... | collective-permute-start | bytes 73736 | tf_op jit(solution)/shard_map/ppermute | solution.py:323
  67.7 4.4 %collective-permute-start.5 = (f32[32,512]{1,0:T(8,128)S(1)}, f32[32,512]{1,0:T(8,128)S(1)}, u32[]{:S(2)}, u32[]{:S(2)}) collective-permute-start(f32[32,512]{1,0:T(8,128)S(1)} %select_maximum_fusion), channel_id=1, source_target_pairs={{0,32},{16,48},{32,0},{48,16},{64,96},{80,112},{96,64},{112,80},{1... | collective-permute-start | bytes 196616 | tf_op jit(solution)/shard_map/ppermute | solution.py:323
  72.0 5.2 %collective-permute-start.6 = (f32[32,256]{1,0:T(8,128)S(1)}, f32[32,256]{1,0:T(8,128)S(1)}, u32[]{:S(2)}, u32[]{:S(2)}) collective-permute-start(f32[32,256]{1,0:T(8,128)S(1)} %slice.153), channel_id=1, source_target_pairs={{0,64},{16,80},{32,96},{48,112},{64,0},{80,16},{96,32},{112,48},{1... | collective-permute-start | bytes 98312 | tf_op jit(solution)/shard_map/ppermute | solution.py:323
  91.0 1.9 %collective-permute-start.7 = (f32[128,1024]{1,0:T(8,128)S(1)}, f32[128,1024]{1,0:T(8,128)S(1)}, u32[]{:S(2)}, u32[]{:S(2)}) collective-permute-start(f32[128,1024]{1,0:T(8,128)S(1)} %bitcast.13), channel_id=1, source_target_pairs={{0,16},{16,0},{32,48},{48,32},{64,80},{80,64},{96,112},{112,96},{1... | collective-permute-start | bytes 1572872 | tf_op jit(solution)/shard_map/ppermute | solution.py:323
  92.9 42.6 %copy-start.4 = (f32[1024,256]{1,0:T(8,128)S(1)}, f32[1024,256]{1,0:T(8,128)}, u32[]{:S(2)}) copy-start(f32[1024,256]{1,0:T(8,128)} %refs_2_.5) | copy-start | bytes 3145732
  96.1 7.4 %collective-permute-start.8 = (f32[16,256]{1,0:T(8,128)S(1)}, f32[16,256]{1,0:T(8,128)S(1)}, u32[]{:S(2)}, u32[]{:S(2)}) collective-permute-start(f32[16,256]{1,0:T(8,128)S(1)} %get-tuple-element.26), channel_id=1, source_target_pairs={{0,64},{16,80},{32,96},{48,112},{64,0},{80,16},{96,32},{112,48},{1... | collective-permute-start | bytes 49160 | tf_op jit(solution)/shard_map/ppermute | solution.py:323
  99.1 5.9 %collective-permute-start.10 = (f32[16,256]{1,0:T(8,128)S(1)}, f32[16,256]{1,0:T(8,128)S(1)}, u32[]{:S(2)}, u32[]{:S(2)}) collective-permute-start(f32[16,256]{1,0:T(8,128)S(1)} %get-tuple-element.26), channel_id=1, source_target_pairs={{0,192},{16,208},{32,224},{48,240},{64,128},{80,144},{96,160},{112... | collective-permute-start | bytes 49160 | tf_op jit(solution)/shard_map/ppermute | solution.py:323
  102.6 7.7 %collective-permute-start.9 = (f32[24,256]{1,0:T(8,128)S(1)}, f32[24,256]{1,0:T(8,128)S(1)}, u32[]{:S(2)}, u32[]{:S(2)}) collective-permute-start(f32[24,256]{1,0:T(8,128)S(1)} %pad_maximum_fusion.2), channel_id=1, source_target_pairs={{0,128},{16,144},{32,160},{48,176},{64,192},{80,208},{96,224},{112... | collective-permute-start | bytes 73736 | tf_op jit(solution)/shard_map/ppermute | solution.py:323
  110.4 25.0 %copy-start.3 = (f32[1024,256]{1,0:T(8,128)S(1)}, f32[1024,256]{1,0:T(8,128)}, u32[]{:S(2)}) copy-start(f32[1024,256]{1,0:T(8,128)} %refs_3_.5) | copy-start | bytes 3145732
  110.6 24.9 %copy-start.1 = (f32[1024,256]{1,0:T(8,128)S(1)}, f32[1024,256]{1,0:T(8,128)}, u32[]{:S(2)}) copy-start(f32[1024,256]{1,0:T(8,128)} %refs_1_.5) | copy-start | bytes 3145732
  110.6 24.9 %copy-start.2 = (f32[1024,256]{1,0:T(8,128)S(1)}, f32[1024,256]{1,0:T(8,128)}, u32[]{:S(2)}) copy-start(f32[1024,256]{1,0:T(8,128)} %refs_0_.5) | copy-start | bytes 3145732
  132.4 3.0 %collective-permute-start.11 = (f32[128,2560]{1,0:T(8,128)S(1)}, f32[128,2560]{1,0:T(8,128)S(1)}, u32[]{:S(2)}, u32[]{:S(2)}) collective-permute-start(f32[128,2560]{1,0:T(8,128)S(1)} %bitcast.11), channel_id=1, source_target_pairs={{0,16},{16,0},{32,48},{48,32},{64,80},{80,64},{96,112},{112,96},{1... | collective-permute-start | bytes 3932168 | tf_op jit(solution)/shard_map/ppermute | solution.py:323

commit v2 on v1

--- a/solution.py
+++ b/solution.py
@@ -183,7 +183,8 @@
     next_ref[...] = own_ref[:, rank : rank + upper] - mm3(cut(ans), cut(full[:, upper_at : upper_at + upper]))
 
 
-def solve_kernel(at, core_ref, mine_ref, theirs_ref, couple_ref, far_ref, y_ref, up_ref, full, n, e):
+def solve_kernel(at, core_ref, mine_ref, theirs_ref, couple_ref, far_ref, y_ref, *refs):
+    full, n, e = refs[-3:]
     rank = full.shape[0]
     gram_at, upper_at, upper, gram_o_at, spot_at = at
     place(core_ref, mine_ref, theirs_ref, full)
@@ -192,7 +193,8 @@
     n[...] = mm3(cut(mm3(cut(full[:, gram_at : gram_at + rank]), cut(couple))), cut(far))
     couple_ref[...] = couple
     far_ref[...] = far
-    up_ref[...] = full[:, upper_at : upper_at + upper]
+    if upper:
+        refs[0][...] = full[:, upper_at : upper_at + upper]
     inverse_into(n, y_ref, e)
 
 
@@ -200,11 +202,12 @@
     rank, upper = 2 * mine.shape[0], at[2]
     vm = pl.BlockSpec(memory_space=pltpu.VMEM)
     square = jax.ShapeDtypeStruct((rank, rank), F32)
+    tail = (jax.ShapeDtypeStruct((rank, upper), F32),) if upper else ()
     return pl.pallas_call(
         functools.partial(solve_kernel, at),
-        out_shape=(square, square, square, jax.ShapeDtypeStruct((rank, upper), F32)),
+        out_shape=(square,) * 3 + tail,
         in_specs=[pl.BlockSpec(memory_space=pltpu.SMEM), vm, vm],
-        out_specs=(vm, vm, vm, vm),
+        out_specs=(vm,) * (3 + len(tail)),
         scratch_shapes=[pltpu.VMEM((rank, mine.shape[1]), F32)] + [pltpu.VMEM((rank, rank), F32)] * 2,
         cost_estimate=pl.CostEstimate(
             flops=60 * 2 * rank**3, bytes_accessed=4 * rank * mine.shape[1], transcendentals=rank * rank
@@ -262,22 +265,18 @@
     )(core, mine, theirs, own, other)
 
 
-def top_kernel(core_ref, mine_ref, theirs_ref, *refs):
+def top_kernel(core_ref, couple_ref, far_ref, y_ref, mine_ref, theirs_ref, *refs):
     held, out_ref = refs[:4], refs[4]
-    full, n, y, e, stacked, result, go = refs[5:]
+    full, stacked, result, go = refs[5:]
     rank = full.shape[0]
     place(core_ref, mine_ref, theirs_ref, full)
     part = lambda k: full[:, k * rank : (k + 1) * rank]
-    couple = couple_of(spots_of(mine_ref, theirs_ref, 4 * rank))
-    couple_t = jnp.transpose(couple)
-    c, c_t = cut(couple), cut(couple_t)
-    far = cut(mm3(cut(part(2)), c_t))
-    n[...] = mm3(cut(mm3(cut(part(0)), c)), far)
-    inverse_into(n, y, e)
-    target = mm3(cut(part(3)), c_t) - mm3(cut(mm3(cut(part(1)), c)), far)
-    top = cut(mm3(cut(target), cut(y[...])))
-    mid = cut(part(6) - mm3(top, cut(part(5))))
-    low = cut(part(9) - mm3(top, cut(part(8))) - mm3(mid, cut(part(7))))
+    couple = couple_ref[...]
+    near = mm3(cut(part(0)), cut(couple))
+    target = mm3(cut(part(1)), cut(couple), dot_t) - mm3(cut(near), cut(far_ref[...]))
+    top = cut(mm3(cut(target), cut(y_ref[...])))
+    mid = cut(part(3) - mm3(top, cut(part(2))))
+    low = cut(part(6) - mm3(top, cut(part(5))) - mm3(mid, cut(part(4))))
     for k, (one, two) in enumerate((top, mid, low)):
         stacked[0, :, k * rank : (k + 1) * rank] = one
         stacked[1, :, k * rank : (k + 1) * rank] = two
@@ -297,7 +296,7 @@
         store.wait()
 
 
-def call_top(core, mine, theirs, carry):
+def call_top(core, solved, mine, theirs, carry):
     rank = 2 * mine.shape[0]
     rows = carry[0].shape[0]
     vm = pl.BlockSpec(memory_space=pltpu.VMEM)
@@ -305,17 +304,16 @@
     return pl.pallas_call(
         top_kernel,
         out_shape=jax.ShapeDtypeStruct((rows, rank), F32),
-        in_specs=[pl.BlockSpec(memory_space=pltpu.SMEM), vm] * 1 + [vm] * 5,
+        in_specs=[pl.BlockSpec(memory_space=pltpu.SMEM)] + [vm] * 9,
         out_specs=far,
         scratch_shapes=[pltpu.VMEM((rank, mine.shape[1]), F32)]
-        + [pltpu.VMEM((rank, rank), F32)] * 3
         + [pltpu.VMEM((2, rank, 3 * rank), jnp.bfloat16), pltpu.VMEM((rows, rank), F32)]
         + [pltpu.SemaphoreType.DMA((4,))],
         cost_estimate=pl.CostEstimate(
             flops=100 * 2 * rank**3, bytes_accessed=4 * rank * mine.shape[1] + 20 * rows * rank, transcendentals=rank * rank
         ),
         compiler_params=pltpu.CompilerParams(vmem_limit_bytes=32 * 1024 * 1024),
-    )(core, mine, theirs, *carry)
+    )(core, *solved, mine, theirs, *carry)
 
 
 def swap(value, mask):
@@ -388,8 +386,9 @@
 
     marks = jnp.concatenate([pick_mid, pick_top, zero2], 0)
     mid = jnp.concatenate([mid, jnp.concatenate([marks, jnp.zeros_like(marks)], 1)], 0)
-    mid = mid + swap(mid, 2)
-    mid_o = swap(mid[:, :rank], 4)
+    part = mid[:, :rank]
+    near, far1, far2 = swap(mid, 2), swap(part, 4), swap(part, 6)
+    mid, mid_o = mid + near, far1 + far2
     marks, marks_o = mid[3 * each :, :rank], mid_o[3 * each :]
     spots = jnp.concatenate([marks[:3], marks_o[:3], zero2], 0)
     marks = marks + marks_o
@@ -402,11 +401,14 @@
     far1, far2 = swap(jnp.concatenate([top, marks], 0), 8), swap(top, 12)
     top, top_o = top + swap(top, 4), far1[: 2 * each] + far2
     spots = jnp.concatenate([marks[3:6], far1[2 * each + 3 : 2 * each + 6], zero2], 0)
-    blocks = [top[:each], top[each:], top_o[:each], top_o[each:], spots]
+    blocks = [top[:each], top_o[:each], spots, top[each:], top_o[each:]]
     blocks += [ans[:each], ans[each:], low[:each], low[each : 2 * each], low[2 * each :]]
     mine = spread_to_all(jnp.concatenate(blocks, 1))
-    theirs = swap(mine, 1)
-    return call_top(core_arg, mine, theirs, (leaf_solved, solved_top, solved_mid, solved_low))
+    early, late = mine[:, : 3 * rank], mine[:, 3 * rank :]
+    early_o = swap(early, 1)
+    late_o = swap(late, 1)
+    solved = call_solve(core_arg, early, early_o, (0, 0, 0, rank, 2 * rank))
+    return call_top(core_arg, solved, late, late_o, (leaf_solved, solved_top, solved_mid, solved_low))
 
 
 def solution(mesh):

time: 144 us -> 143 us (level)
  the two profiles are of different devices: /device:TPU:32 before, /device:TPU:1 now
where the time goes in v2:
time: 143 us
  blocking collectives  54.8 us (38%)
  starting transfers between devices  32.8 us (23%)
  waiting for transfers between devices  24 us (17%)
  Pallas kernels  23.6 us (17%)
  other arithmetic  3.62 us (3%)
  local copies, waits for them, and re-layouts  1.87 us (1%)
  matrix products  1.54 us (1%)
    all_to_all x3, blocking collectives, exchanged(): return lax.all_to_all(pieces, 'pts', 0, 0, tiled=True)  54.8 us
    ppermute x14, starting transfers between devices, swap(): return lax.ppermute(value, 'leaf', [(i, i ^ mask) for i in range(count)])  27.7 us
    ppermute x14, waiting for transfers between devices, swap(): return lax.ppermute(value, 'leaf', [(i, i ^ mask) for i in range(count)])  15.4 us
    pallas_call x2, Pallas kernels, call_product(): pl.pallas_call(functools.partial(product_kernel, count), out_shape=(half,...  10.9 us
    all_to_all x1, waiting for transfers between devices, exchanged(): return lax.all_to_all(pieces, 'pts', 0, 0, tiled=True)  8.55 us
    pallas_call x2, Pallas kernels, call_solve(): pl.pallas_call(functools.partial(solve_kernel, at), out_shape=(square,) *...  5.21 us
    all_to_all x1, starting transfers between devices, exchanged(): return lax.all_to_all(pieces, 'pts', 0, 0, tiled=True)  5.05 us
    pallas_call x1, Pallas kernels, call_top(): pl.pallas_call(top_kernel, out_shape=jax.ShapeDtypeStruct((rows, rank), F...  3.47 us
  transfers between devices with their start and end apart: 15, of which 9 were waited for; matrix products, arithmetic and copies ran while one was open for 4% of the time, Pallas kernels for 7%

profile of v2, /device:TPU:1, one launch (start us, length us, event | category | flops | bytes accessed | tf_op | source)
XLA Modules:
  0.0 142.9 jit_solution(13511516001594556857)
XLA Ops:
  0.0 5.4 %shard_map.109 = (f32[16,8,1536]{2,1,0:T(8,128)S(1)}, f32[16,8,1536]{2,1,0:T(8,128)S(1)}) custom-call(s32[1]{0:T(128)} %bitcast.core_ref, f32[1024,256]{1,0:T(8,128)} %refs_3_.5, f32[1024,256]{1,0:T(8,128)} %refs_2_.5, f32[1024,256]{1,0:T(8,128)} %refs_2_.4, f32[1024,256]{1,0:T(8,128)} %refs_3_.4, f32[1024,256]{1,0:T(8,128)} %refs_4_.3), custom_call_target="tpu_custom_call" | custom-call | flops 2415919104 | bytes 5242880 | tf_op jit(solution)/shard_map/pallas_call | solution.py:73
  5.5 3.3 %collective-permute-start = (f32[16,8,1536]{2,1,0:T(8,128)S(1)}, f32[16,8,1536]{2,1,0:T(8,128)}, u32[]{:S(2)}, u32[]{:S(2)}) collective-permute-start(f32[16,8,1536]{2,1,0:T(8,128)S(1)} %get-tuple-element.21), channel_id=1, source_target_pairs={{0,16},{16,0},{32,48},{48,32},{64,80},{80,64},{96,112},{112,96},{1... | collective-permute-start | bytes 2359304 | tf_op jit(solution)/shard_map/ppermute | solution.py:321
  8.7 5.4 %shard_map.110 = (f32[16,8,1536]{2,1,0:T(8,128)S(1)}, f32[16,8,1536]{2,1,0:T(8,128)S(1)}) custom-call(s32[1]{0:T(128)} %bitcast.core_ref, f32[1024,256]{1,0:T(8,128)} %refs_1_.5, f32[1024,256]{1,0:T(8,128)} %refs_0_.5, f32[1024,256]{1,0:T(8,128)} %refs_2_.4, f32[1024,256]{1,0:T(8,128)} %refs_3_.4, f32[1024,256]{1,0:T(8,128)} %refs_4_.3), custom_call_target="tpu_custom_call" | custom-call | flops 2415919104 | bytes 5242880 | tf_op jit(solution)/shard_map/pallas_call | solution.py:73
  14.4 2.1 %add.48 = f32[16,8,1536]{2,1,0:T(8,128)} add(f32[16,8,1536]{2,1,0:T(8,128)S(1)} %get-tuple-element.20, f32[16,8,1536]{2,1,0:T(8,128)} %collective-permute-done) | non-fusion elementwise | flops 196608 | bytes 2359296 | tf_op jit(solution)/shard_map/add | solution.py:360
  16.5 5.0 %all-to-all-start = ((f32[16,8,1536]{2,1,0:T(8,128)}), f32[16,8,1536]{2,1,0:T(8,128)S(1)}, u32[]{:S(2)}, u32[]{:S(2)}) async-start(f32[16,8,1536]{2,1,0:T(8,128)} %add.48), calls=%async_computation | async-start | bytes 1572864 | tf_op jit(solution)/shard_map/all_to_all | solution.py:329
  25.8 8.6 %all-to-all-done = f32[16,8,1536]{2,1,0:T(8,128)S(1)} async-done(((f32[16,8,1536]{2,1,0:T(8,128)}), f32[16,8,1536]{2,1,0:T(8,128)S(1)}, u32[]{:S(2)}, u32[]{:S(2)}) %all-to-all-start) | async-done | bytes 786464 | tf_op jit(solution)/shard_map/all_to_all | solution.py:329
  34.4 1.7 %collective-permute-start.1 = (f32[8,512]{1,0:T(8,128)S(1)}, f32[8,512]{1,0:T(8,128)S(1)}, u32[]{:S(2)}, u32[]{:S(2)}) collective-permute-start(f32[8,512]{1,0:T(8,128)S(1)} %select_maximum_fusion.1), channel_id=1, source_target_pairs={{0,32},{16,48},{32,0},{48,16},{64,96},{80,112},{96,64},{112,80},{1... | collective-permute-start | bytes 49160 | tf_op jit(solution)/shard_map/ppermute | solution.py:321
  37.4 21.9 %all_to_all.20 = f32[16,8,2816]{2,1,0:T(8,128)S(1)} all-to-all(f32[16,8,2816]{2,1,0:T(8,128)S(1)} %pad_maximum_fusion), channel_id=1, replica_groups=mesh['leaf'=16,'pts'=16] {'pts'}, dimensions={0} | all-to-all | bytes 2883584 | tf_op jit(solution)/shard_map/all_to_all | solution.py:329
  59.4 4.2 %collective-permute-start.3 = (f32[128,1280]{1,0:T(8,128)S(1)}, f32[128,1280]{1,0:T(8,128)S(1)}, u32[]{:S(2)}, u32[]{:S(2)}) collective-permute-start(f32[128,1280]{1,0:T(8,128)S(1)} %slice_bitcast_fusion.mine_ref), channel_id=1, source_target_pairs={{0,16},{16,0},{32,48},{48,32},{64,80},{80,64},{96,112},{112,96},{1... | collective-permute-start | bytes 1966088 | tf_op jit(solution)/shard_map/ppermute | solution.py:321
  65.3 2.7 %shard_map.111 = (f32[256,256]{1,0:T(8,128)S(1)}, f32[256,256]{1,0:T(8,128)S(1)}, f32[256,256]{1,0:T(8,128)S(1)}, f32[256,512]{1,0:T(8,128)S(1)}) custom-call(s32[1]{0:T(128)} %bitcast.core_ref, f32[128,1280]{1,0:T(8,128)S(1)} %slice_bitcast_fusion.mine_ref, f32[128,1280]{1,0:T(8,128)S(1)} %collective-permute-done.3.theirs_ref), custom_call_target="tpu_custom_call" | custom-call | flops 2013265920 | bytes 1310720 | tf_op jit(solution)/shard_map/pallas_call | solution.py:206
  69.0 1.5 %collective-permute-start.5 = (f32[32,512]{1,0:T(8,128)S(1)}, f32[32,512]{1,0:T(8,128)S(1)}, u32[]{:S(2)}, u32[]{:S(2)}) collective-permute-start(f32[32,512]{1,0:T(8,128)S(1)} %select_maximum_fusion), channel_id=1, source_target_pairs={{0,32},{16,48},{32,0},{48,16},{64,96},{80,112},{96,64},{112,80},{1... | collective-permute-start | bytes 196616 | tf_op jit(solution)/shard_map/ppermute | solution.py:321
  70.5 2.8 %collective-permute-start.7 = (f32[32,256]{1,0:T(8,128)S(1)}, f32[32,256]{1,0:T(8,128)S(1)}, u32[]{:S(2)}, u32[]{:S(2)}) collective-permute-start(f32[32,256]{1,0:T(8,128)S(1)} %slice.161), channel_id=1, source_target_pairs={{0,96},{16,112},{32,64},{48,80},{64,32},{80,48},{96,0},{112,16},{1... | collective-permute-start | bytes 98312 | tf_op jit(solution)/shard_map/ppermute | solution.py:321
  73.5 1.9 %collective-permute-done.7 = f32[32,256]{1,0:T(8,128)S(1)} collective-permute-done((f32[32,256]{1,0:T(8,128)S(1)}, f32[32,256]{1,0:T(8,128)S(1)}, u32[]{:S(2)}, u32[]{:S(2)}) %collective-permute-start.7) | collective-permute-done | bytes 32800 | tf_op jit(solution)/shard_map/ppermute | solution.py:321
  75.4 1.9 %collective-permute-done.6 = f32[32,256]{1,0:T(8,128)S(1)} collective-permute-done((f32[32,256]{1,0:T(8,128)S(1)}, f32[32,256]{1,0:T(8,128)S(1)}, u32[]{:S(2)}, u32[]{:S(2)}) %collective-permute-start.6) | collective-permute-done | bytes 32800 | tf_op jit(solution)/shard_map/ppermute | solution.py:321
  77.5 12.5 %all_to_all.21 = f32[16,8,1024]{2,1,0:T(8,128)S(1)} all-to-all(f32[16,8,1024]{2,1,0:T(8,128)S(1)} %broadcast_in_dim.18), channel_id=1, replica_groups=mesh['leaf'=16,'pts'=16] {'pts'}, dimensions={0} | all-to-all | bytes 1048576 | tf_op jit(solution)/shard_map/all_to_all | solution.py:329
  89.9 3.2 %collective-permute-start.8 = (f32[128,1024]{1,0:T(8,128)S(1)}, f32[128,1024]{1,0:T(8,128)S(1)}, u32[]{:S(2)}, u32[]{:S(2)}) collective-permute-start(f32[128,1024]{1,0:T(8,128)S(1)} %bitcast.11), channel_id=1, source_target_pairs={{0,16},{16,0},{32,48},{48,32},{64,80},{80,64},{96,112},{112,96},{1... | collective-permute-start | bytes 1572872 | tf_op jit(solution)/shard_map/ppermute | solution.py:321
  94.7 3.2 %shard_map.113 = (f32[16,256]{1,0:T(8,128)S(1)}, f32[16,256]{1,0:T(8,128)S(1)}) custom-call(s32[1]{0:T(128)} %bitcast.core_ref, f32[128,1024]{1,0:T(8,128)S(1)} %bitcast.12, f32[128,1024]{1,0:T(8,128)S(1)} %collective-permute-done.8.theirs_ref, f32[16,512]{1,0:T(8,128)S(1)} %slice.165.own_ref, f32[16,256]{1,0:T(8,128)S(1)} %slice.166.other_ref), custom_call_target="tpu_custom_call" | custom-call | flops 2684354560 | bytes 1048576 | tf_op jit(solution)/shard_map/pallas_call | solution.py:252
  97.9 5.4 %collective-permute-start.11 = (f32[16,256]{1,0:T(8,128)S(1)}, f32[16,256]{1,0:T(8,128)S(1)}, u32[]{:S(2)}, u32[]{:S(2)}) collective-permute-start(f32[16,256]{1,0:T(8,128)S(1)} %get-tuple-element.29), channel_id=1, source_target_pairs={{0,192},{16,208},{32,224},{48,240},{64,128},{80,144},{96,160},{112... | collective-permute-start | bytes 49160 | tf_op jit(solution)/shard_map/ppermute | solution.py:321
  104.5 5.5 %collective-permute-done.10 = f32[24,256]{1,0:T(8,128)S(1)} collective-permute-done((f32[24,256]{1,0:T(8,128)S(1)}, f32[24,256]{1,0:T(8,128)S(1)}, u32[]{:S(2)}, u32[]{:S(2)}) %collective-permute-start.10) | collective-permute-done | bytes 24608 | tf_op jit(solution)/shard_map/ppermute | solution.py:321
  110.2 20.4 %all_to_all.22 = f32[16,8,2560]{2,1,0:T(8,128)S(1)} all-to-all(f32[16,8,2560]{2,1,0:T(8,128)S(1)} %broadcast_in_dim.19), channel_id=1, replica_groups=mesh['leaf'=16,'pts'=16] {'pts'}, dimensions={0} | all-to-all | bytes 2621440 | tf_op jit(solution)/shard_map/all_to_all | solution.py:329
  130.6 3.3 %collective-permute-start.13 = (f32[128,1792]{1,0:T(8,128)S(1)}, f32[128,1792]{1,0:T(8,128)S(1)}, u32[]{:S(2)}, u32[]{:S(2)}) collective-permute-start(f32[128,1792]{1,0:T(8,128)S(1)} %slice.177.mine_ref), channel_id=1, source_target_pairs={{0,16},{16,0},{32,48},{48,32},{64,80},{80,64},{96,112},{112,96},{1... | collective-permute-start | bytes 2752520 | tf_op jit(solution)/shard_map/ppermute | solution.py:321
  134.2 2.5 %collective-permute-done.12.theirs_ref = f32[128,768]{1,0:T(8,128)S(1)} collective-permute-done((f32[128,768]{1,0:T(8,128)S(1)}, f32[128,768]{1,0:T(8,128)S(1)}, u32[]{:S(2)}, u32[]{:S(2)}) %collective-permute-start.12) | collective-permute-done | bytes 393248 | tf_op jit(solution)/shard_map/ppermute | solution.py:321
  136.7 2.5 %shard_map.114 = (f32[256,256]{1,0:T(8,128)S(1)}, f32[256,256]{1,0:T(8,128)S(1)}, f32[256,256]{1,0:T(8,128)S(1)}) custom-call(s32[1]{0:T(128)} %bitcast.core_ref, f32[128,768]{1,0:T(8,128)S(1)} %slice.176.mine_ref, f32[128,768]{1,0:T(8,128)S(1)} %collective-permute-done.12.theirs_ref), custom_call_target="tpu_custom_call" | custom-call | flops 2013265920 | bytes 786432 | tf_op jit(solution)/shard_map/pallas_call | solution.py:206
  139.2 3.5 %shard_map.115 = f32[1024,256]{1,0:T(8,128)} custom-call(s32[1]{0:T(128)} %bitcast.core_ref, f32[256,256]{1,0:T(8,128)S(1)} %get-tuple-element.32.couple_ref, f32[256,256]{1,0:T(8,128)S(1)} %get-tuple-element.33.far_ref, f32[256,256]{1,0:T(8,128)S(1)} %get-tuple-element.34.y_ref, f32[128,1792]{1,0:T(8,128)S(1)} %slice.177.mine_ref, ...), custom_call_target="tpu_custom_call" | custom-call | flops 3355443200 | bytes 7077888 | tf_op jit(solution)/shard_map/pallas_call | solution.py:304
  (82 shorter events, 11.7 us)
Async XLA Ops:
  0.0 23.0 %copy-start = (f32[3,1024]{1,0:T(4,128)S(1)}, f32[3,1024]{1,0:T(4,128)}, u32[]{:S(2)}) copy-start(f32[3,1024]{1,0:T(4,128)} %param.12) | copy-start | bytes 36868
  5.5 8.9 %copy-start.5 = (s32[2,256]{1,0:T(2,128)S(1)}, s32[2,256]{1,0:T(2,128)}, u32[]{:S(2)}) copy-start(s32[2,256]{1,0:T(2,128)} %param.19) | copy-start | bytes 6148
  5.5 8.9 %collective-permute-start = (f32[16,8,1536]{2,1,0:T(8,128)S(1)}, f32[16,8,1536]{2,1,0:T(8,128)}, u32[]{:S(2)}, u32[]{:S(2)}) collective-permute-start(f32[16,8,1536]{2,1,0:T(8,128)S(1)} %get-tuple-element.21), channel_id=1, source_target_pairs={{0,16},{16,0},{32,48},{48,32},{64,80},{80,64},{96,112},{112,96},{1... | collective-permute-start | bytes 2359304 | tf_op jit(solution)/shard_map/ppermute | solution.py:321
  14.2 10.3 %collective-permute-start.2 = (f32[16,8,1536]{2,1,0:T(8,128)S(1)}, f32[16,8,1536]{2,1,0:T(8,128)}, u32[]{:S(2)}, u32[]{:S(2)}) collective-permute-start(f32[16,8,1536]{2,1,0:T(8,128)S(1)} %get-tuple-element.23), channel_id=1, source_target_pairs={{0,16},{16,0},{32,48},{48,32},{64,80},{80,64},{96,112},{112,96},{1... | collective-permute-start | bytes 2359304 | tf_op jit(solution)/shard_map/ppermute | solution.py:321
  16.5 17.8 %all-to-all-start = ((f32[16,8,1536]{2,1,0:T(8,128)}), f32[16,8,1536]{2,1,0:T(8,128)S(1)}, u32[]{:S(2)}, u32[]{:S(2)}) async-start(f32[16,8,1536]{2,1,0:T(8,128)} %add.48), calls=%async_computation | async-start | bytes 1572864 | tf_op jit(solution)/shard_map/all_to_all | solution.py:329
  34.4 2.8 %collective-permute-start.1 = (f32[8,512]{1,0:T(8,128)S(1)}, f32[8,512]{1,0:T(8,128)S(1)}, u32[]{:S(2)}, u32[]{:S(2)}) collective-permute-start(f32[8,512]{1,0:T(8,128)S(1)} %select_maximum_fusion.1), channel_id=1, source_target_pairs={{0,32},{16,48},{32,0},{48,16},{64,96},{80,112},{96,64},{112,80},{1... | collective-permute-start | bytes 49160 | tf_op jit(solution)/shard_map/ppermute | solution.py:321
  59.4 5.9 %collective-permute-start.3 = (f32[128,1280]{1,0:T(8,128)S(1)}, f32[128,1280]{1,0:T(8,128)S(1)}, u32[]{:S(2)}, u32[]{:S(2)}) collective-permute-start(f32[128,1280]{1,0:T(8,128)S(1)} %slice_bitcast_fusion.mine_ref), channel_id=1, source_target_pairs={{0,16},{16,0},{32,48},{48,32},{64,80},{80,64},{96,112},{112,96},{1... | collective-permute-start | bytes 1966088 | tf_op jit(solution)/shard_map/ppermute | solution.py:321
  63.7 4.3 %collective-permute-start.4 = (f32[24,256]{1,0:T(8,128)S(1)}, f32[24,256]{1,0:T(8,128)S(1)}, u32[]{:S(2)}, u32[]{:S(2)}) collective-permute-start(f32[24,256]{1,0:T(8,128)S(1)} %slice.157), channel_id=1, source_target_pairs={{0,32},{16,48},{32,0},{48,16},{64,96},{80,112},{96,64},{112,80},{1... | collective-permute-start | bytes 73736 | tf_op jit(solution)/shard_map/ppermute | solution.py:321
  69.0 8.4 %collective-permute-start.5 = (f32[32,512]{1,0:T(8,128)S(1)}, f32[32,512]{1,0:T(8,128)S(1)}, u32[]{:S(2)}, u32[]{:S(2)}) collective-permute-start(f32[32,512]{1,0:T(8,128)S(1)} %select_maximum_fusion), channel_id=1, source_target_pairs={{0,32},{16,48},{32,0},{48,16},{64,96},{80,112},{96,64},{112,80},{1... | collective-permute-start | bytes 196616 | tf_op jit(solution)/shard_map/ppermute | solution.py:321
  70.5 4.9 %collective-permute-start.7 = (f32[32,256]{1,0:T(8,128)S(1)}, f32[32,256]{1,0:T(8,128)S(1)}, u32[]{:S(2)}, u32[]{:S(2)}) collective-permute-start(f32[32,256]{1,0:T(8,128)S(1)} %slice.161), channel_id=1, source_target_pairs={{0,96},{16,112},{32,64},{48,80},{64,32},{80,48},{96,0},{112,16},{1... | collective-permute-start | bytes 98312 | tf_op jit(solution)/shard_map/ppermute | solution.py:321
  73.3 4.0 %collective-permute-start.6 = (f32[32,256]{1,0:T(8,128)S(1)}, f32[32,256]{1,0:T(8,128)S(1)}, u32[]{:S(2)}, u32[]{:S(2)}) collective-permute-start(f32[32,256]{1,0:T(8,128)S(1)} %slice.161), channel_id=1, source_target_pairs={{0,64},{16,80},{32,96},{48,112},{64,0},{80,16},{96,32},{112,48},{1... | collective-permute-start | bytes 98312 | tf_op jit(solution)/shard_map/ppermute | solution.py:321
  89.9 4.8 %collective-permute-start.8 = (f32[128,1024]{1,0:T(8,128)S(1)}, f32[128,1024]{1,0:T(8,128)S(1)}, u32[]{:S(2)}, u32[]{:S(2)}) collective-permute-start(f32[128,1024]{1,0:T(8,128)S(1)} %bitcast.11), channel_id=1, source_target_pairs={{0,16},{16,0},{32,48},{48,32},{64,80},{80,64},{96,112},{112,96},{1... | collective-permute-start | bytes 1572872 | tf_op jit(solution)/shard_map/ppermute | solution.py:321
  97.9 5.7 %collective-permute-start.9 = (f32[16,256]{1,0:T(8,128)S(1)}, f32[16,256]{1,0:T(8,128)S(1)}, u32[]{:S(2)}, u32[]{:S(2)}) collective-permute-start(f32[16,256]{1,0:T(8,128)S(1)} %get-tuple-element.29), channel_id=1, source_target_pairs={{0,64},{16,80},{32,96},{48,112},{64,0},{80,16},{96,32},{112,48},{1... | collective-permute-start | bytes 49160 | tf_op jit(solution)/shard_map/ppermute | solution.py:321
  97.9 6.5 %collective-permute-start.11 = (f32[16,256]{1,0:T(8,128)S(1)}, f32[16,256]{1,0:T(8,128)S(1)}, u32[]{:S(2)}, u32[]{:S(2)}) collective-permute-start(f32[16,256]{1,0:T(8,128)S(1)} %get-tuple-element.29), channel_id=1, source_target_pairs={{0,192},{16,208},{32,224},{48,240},{64,128},{80,144},{96,160},{112... | collective-permute-start | bytes 49160 | tf_op jit(solution)/shard_map/ppermute | solution.py:321
  103.3 6.6 %collective-permute-start.10 = (f32[24,256]{1,0:T(8,128)S(1)}, f32[24,256]{1,0:T(8,128)S(1)}, u32[]{:S(2)}, u32[]{:S(2)}) collective-permute-start(f32[24,256]{1,0:T(8,128)S(1)} %pad_maximum_fusion.2), channel_id=1, source_target_pairs={{0,128},{16,144},{32,160},{48,176},{64,192},{80,208},{96,224},{112... | collective-permute-start | bytes 73736 | tf_op jit(solution)/shard_map/ppermute | solution.py:321
  130.6 8.5 %collective-permute-start.13 = (f32[128,1792]{1,0:T(8,128)S(1)}, f32[128,1792]{1,0:T(8,128)S(1)}, u32[]{:S(2)}, u32[]{:S(2)}) collective-permute-start(f32[128,1792]{1,0:T(8,128)S(1)} %slice.177.mine_ref), channel_id=1, source_target_pairs={{0,16},{16,0},{32,48},{48,32},{64,80},{80,64},{96,112},{112,96},{1... | collective-permute-start | bytes 2752520 | tf_op jit(solution)/shard_map/ppermute | solution.py:321
  134.0 5.2 %copy-start.1 = (f32[1024,256]{1,0:T(8,128)S(1)}, f32[1024,256]{1,0:T(8,128)}, u32[]{:S(2)}) copy-start(f32[1024,256]{1,0:T(8,128)} %refs_1_.5) | copy-start | bytes 3145732
  134.0 5.2 %copy-start.2 = (f32[1024,256]{1,0:T(8,128)S(1)}, f32[1024,256]{1,0:T(8,128)}, u32[]{:S(2)}) copy-start(f32[1024,256]{1,0:T(8,128)} %refs_0_.5) | copy-start | bytes 3145732
  134.0 5.2 %copy-start.3 = (f32[1024,256]{1,0:T(8,128)S(1)}, f32[1024,256]{1,0:T(8,128)}, u32[]{:S(2)}) copy-start(f32[1024,256]{1,0:T(8,128)} %refs_3_.5) | copy-start | bytes 3145732
  134.1 5.2 %copy-start.4 = (f32[1024,256]{1,0:T(8,128)S(1)}, f32[1024,256]{1,0:T(8,128)}, u32[]{:S(2)}) copy-start(f32[1024,256]{1,0:T(8,128)} %refs_2_.5) | copy-start | bytes 3145732
  134.1 2.6 %collective-permute-start.12 = (f32[128,768]{1,0:T(8,128)S(1)}, f32[128,768]{1,0:T(8,128)S(1)}, u32[]{:S(2)}, u32[]{:S(2)}) collective-permute-start(f32[128,768]{1,0:T(8,128)S(1)} %slice.176.mine_ref), channel_id=1, source_target_pairs={{0,16},{16,0},{32,48},{48,32},{64,80},{80,64},{96,112},{112,96},{1... | collective-permute-start | bytes 1179656 | tf_op jit(solution)/shard_map/ppermute | solution.py:321
